TPU v7x, 32 devices: a whole 2x2x4 slice. The times are simulated.
32 devices in a mesh: tm: 8 (over y, x, core), space: 4 (over z).
Axes of the slice: x: 2, y: 2, z: 4, core: 2. Of those that a mesh axis runs over, the one named last changes fastest.
Arguments:
- trajectory: float32 [64, 256, 1024], P('tm', 'space'), may hold values from -1.2 to 1.2
- initial_state: float32 [256, 1024], P('space'), may hold values from -1 to 1
- residual: float32 [64, 256, 1024], P('tm', 'space'), may hold values from -3000 to 3000
- mobility: float32 [256, 1024], P('space'), may hold values from 20 to 200
Outputs:
- update: float32 [64, 256, 1024], P('tm', 'space')
- reduction: float32 [], replicated
All inputs are finite; a program needn't handle non-finite values.
Results may differ from a plain program's by a relative error of at most 0.00015.
Values sent between devices are 32-bit elements; how exact they have to be, the bound alone decides.
A program may use at most 64 MiB of HBM per device.

v0:
```python
import jax
import jax.numpy as jnp
from jax import lax
from jax.sharding import PartitionSpec as P

NT = 64
SWEEPS = 16


circ_weight = 0.2
time_step = 0.01
damping = 0.8
reaction_scale = 40.0


def padded_2(block, sides, width):
    for axis, dim in sides:
        count = lax.axis_size(axis)
        forward = [(i, i + 1) for i in range(count - 1)]
        forward.append((count - 1, 0))
        backward = [(target, source) for source, target in forward]
        low = lax.ppermute(
            lax.slice_in_dim(block, block.shape[dim] - width, None, axis=dim), axis, forward
        )
        high = lax.ppermute(lax.slice_in_dim(block, 0, width, axis=dim), axis, backward)
        block = jnp.concatenate([low, block, high], axis=dim)
    return block


def passed_along(block, axis, distance):
    devices = range(lax.axis_size(axis))
    route = [(i - distance, i) for i in devices if i - distance in devices]
    return lax.ppermute(block, axis, route)


def time_tables(step_count):
    positions = jnp.arange(step_count).astype(jnp.float32)
    pair_ids = jnp.arange(step_count // 2).astype(jnp.float32)
    phases = 2.0 * jnp.pi * pair_ids / step_count
    angles = phases[:, None] * positions[None, :]
    forward = jnp.stack([jnp.cos(angles), -jnp.sin(angles)], axis=1).reshape(step_count, step_count)
    row_id = jnp.arange(step_count)[:, None]
    forward = jnp.where(row_id == 1, jnp.cos(jnp.pi * positions)[None, :], forward)
    scaling = jnp.where(jnp.arange(step_count) < 2, 1.0, 2.0) / step_count
    inverse = forward.T * scaling[None, :]
    factor = circ_weight ** (1.0 / step_count)
    shift_pair = (1.0 - factor * jnp.cos(phases)) / time_step
    shifts = jnp.stack([shift_pair, shift_pair], axis=1).reshape(step_count)
    shifts = shifts.at[1].set((1.0 + factor) / time_step)
    coupling = factor * jnp.sin(phases) / time_step
    signed = jnp.stack([-coupling, coupling], axis=1).reshape(step_count)
    weights = circ_weight ** (positions / step_count)
    return (forward, inverse, shifts, signed, weights)


def neg_laplace(values):
    padded = padded_2(values, (("space", 1),), 1)
    middle = padded[:, 1:-1, :]
    neighbours = padded[:, 2:, :] + padded[:, :-2, :]
    neighbours = neighbours + jnp.roll(middle, 1, axis=2) + jnp.roll(middle, -1, axis=2)
    return 4.0 * values - neighbours


def partner(values):
    extent = values.shape
    return jnp.flip(values.reshape(extent[0] // 2, 2, extent[1], extent[2]), axis=1).reshape(extent)


def make_sweep(spectrum, shifts, signed, frozen, mobility, laplace_fn):
    shift_col = shifts[:, None, None]
    signed_col = signed[:, None, None]
    diagonal = shift_col + (frozen + 4.0 * mobility)[None]
    partner_diag = partner(diagonal)
    denominator = diagonal * partner_diag + signed_col * signed_col

    def one_sweep(sweep_id, values):
        applied = (
            (shift_col + frozen[None]) * values
            + mobility[None] * laplace_fn(values)
            + signed_col * partner(values)
        )
        defect = spectrum - applied
        return (
            values + damping * (partner_diag * defect - signed_col * partner(defect)) / denominator
        )

    return one_sweep


def relax_pairs(spectrum, shifts, signed, frozen, mobility):
    one_sweep = make_sweep(spectrum, shifts, signed, frozen, mobility, neg_laplace)
    return lax.fori_loop(0, SWEEPS, one_sweep, jnp.zeros_like(spectrum))


def precondition(values, frozen, mobility, tables):
    forward, inverse, shifts, signed, weights = tables
    steps_dev = values.shape[0]
    time_rank = lax.axis_index("tm")
    offset = time_rank * steps_dev
    own_weights = lax.dynamic_slice_in_dim(weights, offset, steps_dev)
    own_shifts = lax.dynamic_slice_in_dim(shifts, offset, steps_dev)
    own_signed = lax.dynamic_slice_in_dim(signed, offset, steps_dev)
    weighted = own_weights[:, None, None] * values
    spectrum = jnp.einsum(
        "mj,jrc->mrc",
        forward,
        lax.all_to_all(weighted, "tm", split_axis=1, concat_axis=0, tiled=True),
        precision=lax.Precision.HIGHEST,
    )
    owned_part = lax.all_to_all(spectrum, "tm", split_axis=0, concat_axis=1, tiled=True)
    solved = relax_pairs(owned_part, own_shifts, own_signed, frozen, mobility)
    in_time = jnp.einsum(
        "jm,mrc->jrc",
        inverse,
        lax.all_to_all(solved, "tm", split_axis=1, concat_axis=0, tiled=True),
        precision=lax.Precision.HIGHEST,
    )
    restored = lax.all_to_all(in_time, "tm", split_axis=0, concat_axis=1, tiled=True)
    return restored / own_weights[:, None, None]


def jacobian(values, trajectory, mobility):
    arriving = passed_along(values[-1:], "tm", 1)
    earlier = jnp.concatenate([arriving, values[:-1]], axis=0)
    reaction = reaction_scale * (3.0 * trajectory * trajectory - 1.0)
    return (values - earlier) / time_step + mobility[None] * neg_laplace(values) + reaction * values


def on_device(trajectory, initial_state, residual, mobility):
    tables = time_tables(NT)
    frozen = reaction_scale * jnp.maximum(3.0 * initial_state * initial_state - 1.0, 0.0)
    direction = precondition(residual, frozen, mobility, tables)
    applied = jacobian(direction, trajectory, mobility)
    norm_square, cross_sum, squared_applied = lax.psum(
        (jnp.sum(residual * residual), jnp.sum(residual * applied), jnp.sum(applied * applied)),
        ("tm", "space"),
    )
    projection = cross_sum / norm_square
    squared_sum = squared_applied / norm_square
    remainder = jnp.maximum(squared_sum - projection * projection, 0.0)
    update = cross_sum / squared_applied * direction
    reduction = jnp.sqrt(remainder / squared_sum)
    return (update, reduction)


def solution(mesh):
    placed = (P("tm", "space", None), P("space", None), P("tm", "space", None), P("space", None))
    return jax.shard_map(
        on_device,
        mesh=mesh,
        in_specs=placed,
        out_specs=(P("tm", "space", None), P()),
        check_vma=False,
    )
```

profile of v0, /device:TPU:0, one launch (start us, length us, event | category | flops | bytes accessed | tf_op | source)
XLA Modules:
  0.0 605.1 jit_solution(17352459910690537960)
XLA Ops:
  10.4 26.3 %all-to-all-done = f32[8,64,1024]{2,0,1:T(8,128)S(1)} async-done(((f32[8,64,1024]{2,0,1:T(8,128)}), f32[8,64,1024]{2,0,1:T(8,128)S(1)}, u32[]{:S(2)}, u32[]{:S(2)}) %all-to-all-start) | async-done | bytes 2097184 | tf_op jit(solution)/shard_map/all_to_all | solution.py:107
  54.1 17.4 %all-to-all-done.1 = f32[64,8,1024]{2,1,0:T(8,128)S(1)} async-done(((f32[64,8,1024]{2,1,0:T(8,128)}), f32[64,8,1024]{2,1,0:T(8,128)S(1)}, u32[]{:S(2)}, u32[]{:S(2)}) %all-to-all-start.1) | async-done | bytes 2097184 | tf_op jit(solution)/shard_map/all_to_all | solution.py:110
  73.0 395.9 %while.12 = (s32[]{:T(128)}, f32[8,64,1024]{2,1,0:T(8,128)}, f32[8,1,1]{0,2,1:T(1,128)S(1)}, f32[64,1024]{1,0:T(8,128)S(1)}, f32[64,1024]{1,0:T(8,128)S(1)}, /*i...) while((s32[]{:T(128)}, f32[8,64,1024]{2,1,0:T(8,128)}, ...), condition=%wide.region_1.2_spmd.clone, body=%wide.region_0.1_spmd.clone.sunk | while | flops 12582915 | bytes 55509316 | solution.py:92
  90.2 5.5 fusion.57
  105.7 5.4 fusion.56
  114.5 6.1 %fusion.57 = f32[8,64,1024]{2,1,0:T(8,128)} fusion(f32[8,64,1024]{2,1,0:T(8,128)} %get-tuple-element.242, f32[4,2,64,1024]{3,2,1,0:T(8,128)} %rev.16, f32[8,64,1024]{2,1,0:T(8,128)} %get-tuple-element.241, f32[8,64,1024]{2,1,0:T(8,128)S(1)} %copy-done, f32[8]{0:T(128)S(1)} %bitcast.80, f32[8,64,1024]{2,1,0:T(8,128)} %get-tuple-element.224, ...), kind=kLoop, calls=%fused_computation.14.clone.1 | loop fusion | flops 3670016 | bytes 12582945 | tf_op jit(solution)/shard_map/while/body/eval_jaxpr/add | solution.py:84
  139.3 6.1 %fusion.57 = f32[8,64,1024]{2,1,0:T(8,128)} fusion(f32[8,64,1024]{2,1,0:T(8,128)} %get-tuple-element.242, f32[4,2,64,1024]{3,2,1,0:T(8,128)} %rev.16, f32[8,64,1024]{2,1,0:T(8,128)} %get-tuple-element.241, f32[8,64,1024]{2,1,0:T(8,128)S(1)} %copy-done, f32[8]{0:T(128)S(1)} %bitcast.80, f32[8,64,1024]{2,1,0:T(8,128)} %get-tuple-element.224, ...), kind=kLoop, calls=%fused_computation.14.clone.1 | loop fusion | flops 3670016 | bytes 12582945 | tf_op jit(solution)/shard_map/while/body/eval_jaxpr/add | solution.py:84
  155.5 5.4 fusion.56
  164.2 6.1 %fusion.57 = f32[8,64,1024]{2,1,0:T(8,128)} fusion(f32[8,64,1024]{2,1,0:T(8,128)} %get-tuple-element.242, f32[4,2,64,1024]{3,2,1,0:T(8,128)} %rev.16, f32[8,64,1024]{2,1,0:T(8,128)} %get-tuple-element.241, f32[8,64,1024]{2,1,0:T(8,128)S(1)} %copy-done, f32[8]{0:T(128)S(1)} %bitcast.80, f32[8,64,1024]{2,1,0:T(8,128)} %get-tuple-element.224, ...), kind=kLoop, calls=%fused_computation.14.clone.1 | loop fusion | flops 3670016 | bytes 12582945 | tf_op jit(solution)/shard_map/while/body/eval_jaxpr/add | solution.py:84
  180.3 5.4 fusion.56
  189.1 6.1 %fusion.57 = f32[8,64,1024]{2,1,0:T(8,128)} fusion(f32[8,64,1024]{2,1,0:T(8,128)} %get-tuple-element.242, f32[4,2,64,1024]{3,2,1,0:T(8,128)} %rev.16, f32[8,64,1024]{2,1,0:T(8,128)} %get-tuple-element.241, f32[8,64,1024]{2,1,0:T(8,128)S(1)} %copy-done, f32[8]{0:T(128)S(1)} %bitcast.80, f32[8,64,1024]{2,1,0:T(8,128)} %get-tuple-element.224, ...), kind=kLoop, calls=%fused_computation.14.clone.1 | loop fusion | flops 3670016 | bytes 12582945 | tf_op jit(solution)/shard_map/while/body/eval_jaxpr/add | solution.py:84
  214.0 6.1 %fusion.57 = f32[8,64,1024]{2,1,0:T(8,128)} fusion(f32[8,64,1024]{2,1,0:T(8,128)} %get-tuple-element.242, f32[4,2,64,1024]{3,2,1,0:T(8,128)} %rev.16, f32[8,64,1024]{2,1,0:T(8,128)} %get-tuple-element.241, f32[8,64,1024]{2,1,0:T(8,128)S(1)} %copy-done, f32[8]{0:T(128)S(1)} %bitcast.80, f32[8,64,1024]{2,1,0:T(8,128)} %get-tuple-element.224, ...), kind=kLoop, calls=%fused_computation.14.clone.1 | loop fusion | flops 3670016 | bytes 12582945 | tf_op jit(solution)/shard_map/while/body/eval_jaxpr/add | solution.py:84
  230.1 5.4 fusion.56
  238.9 6.1 %fusion.57 = f32[8,64,1024]{2,1,0:T(8,128)} fusion(f32[8,64,1024]{2,1,0:T(8,128)} %get-tuple-element.242, f32[4,2,64,1024]{3,2,1,0:T(8,128)} %rev.16, f32[8,64,1024]{2,1,0:T(8,128)} %get-tuple-element.241, f32[8,64,1024]{2,1,0:T(8,128)S(1)} %copy-done, f32[8]{0:T(128)S(1)} %bitcast.80, f32[8,64,1024]{2,1,0:T(8,128)} %get-tuple-element.224, ...), kind=kLoop, calls=%fused_computation.14.clone.1 | loop fusion | flops 3670016 | bytes 12582945 | tf_op jit(solution)/shard_map/while/body/eval_jaxpr/add | solution.py:84
  255.0 5.4 fusion.56
  263.7 6.1 %fusion.57 = f32[8,64,1024]{2,1,0:T(8,128)} fusion(f32[8,64,1024]{2,1,0:T(8,128)} %get-tuple-element.242, f32[4,2,64,1024]{3,2,1,0:T(8,128)} %rev.16, f32[8,64,1024]{2,1,0:T(8,128)} %get-tuple-element.241, f32[8,64,1024]{2,1,0:T(8,128)S(1)} %copy-done, f32[8]{0:T(128)S(1)} %bitcast.80, f32[8,64,1024]{2,1,0:T(8,128)} %get-tuple-element.224, ...), kind=kLoop, calls=%fused_computation.14.clone.1 | loop fusion | flops 3670016 | bytes 12582945 | tf_op jit(solution)/shard_map/while/body/eval_jaxpr/add | solution.py:84
  288.6 6.1 %fusion.57 = f32[8,64,1024]{2,1,0:T(8,128)} fusion(f32[8,64,1024]{2,1,0:T(8,128)} %get-tuple-element.242, f32[4,2,64,1024]{3,2,1,0:T(8,128)} %rev.16, f32[8,64,1024]{2,1,0:T(8,128)} %get-tuple-element.241, f32[8,64,1024]{2,1,0:T(8,128)S(1)} %copy-done, f32[8]{0:T(128)S(1)} %bitcast.80, f32[8,64,1024]{2,1,0:T(8,128)} %get-tuple-element.224, ...), kind=kLoop, calls=%fused_computation.14.clone.1 | loop fusion | flops 3670016 | bytes 12582945 | tf_op jit(solution)/shard_map/while/body/eval_jaxpr/add | solution.py:84
  304.7 5.4 fusion.56
  313.5 6.1 %fusion.57 = f32[8,64,1024]{2,1,0:T(8,128)} fusion(f32[8,64,1024]{2,1,0:T(8,128)} %get-tuple-element.242, f32[4,2,64,1024]{3,2,1,0:T(8,128)} %rev.16, f32[8,64,1024]{2,1,0:T(8,128)} %get-tuple-element.241, f32[8,64,1024]{2,1,0:T(8,128)S(1)} %copy-done, f32[8]{0:T(128)S(1)} %bitcast.80, f32[8,64,1024]{2,1,0:T(8,128)} %get-tuple-element.224, ...), kind=kLoop, calls=%fused_computation.14.clone.1 | loop fusion | flops 3670016 | bytes 12582945 | tf_op jit(solution)/shard_map/while/body/eval_jaxpr/add | solution.py:84
  329.6 5.4 fusion.56
  338.4 6.1 %fusion.57 = f32[8,64,1024]{2,1,0:T(8,128)} fusion(f32[8,64,1024]{2,1,0:T(8,128)} %get-tuple-element.242, f32[4,2,64,1024]{3,2,1,0:T(8,128)} %rev.16, f32[8,64,1024]{2,1,0:T(8,128)} %get-tuple-element.241, f32[8,64,1024]{2,1,0:T(8,128)S(1)} %copy-done, f32[8]{0:T(128)S(1)} %bitcast.80, f32[8,64,1024]{2,1,0:T(8,128)} %get-tuple-element.224, ...), kind=kLoop, calls=%fused_computation.14.clone.1 | loop fusion | flops 3670016 | bytes 12582945 | tf_op jit(solution)/shard_map/while/body/eval_jaxpr/add | solution.py:84
  363.2 6.1 %fusion.57 = f32[8,64,1024]{2,1,0:T(8,128)} fusion(f32[8,64,1024]{2,1,0:T(8,128)} %get-tuple-element.242, f32[4,2,64,1024]{3,2,1,0:T(8,128)} %rev.16, f32[8,64,1024]{2,1,0:T(8,128)} %get-tuple-element.241, f32[8,64,1024]{2,1,0:T(8,128)S(1)} %copy-done, f32[8]{0:T(128)S(1)} %bitcast.80, f32[8,64,1024]{2,1,0:T(8,128)} %get-tuple-element.224, ...), kind=kLoop, calls=%fused_computation.14.clone.1 | loop fusion | flops 3670016 | bytes 12582945 | tf_op jit(solution)/shard_map/while/body/eval_jaxpr/add | solution.py:84
  379.4 5.4 fusion.56
  388.1 6.1 %fusion.57 = f32[8,64,1024]{2,1,0:T(8,128)} fusion(f32[8,64,1024]{2,1,0:T(8,128)} %get-tuple-element.242, f32[4,2,64,1024]{3,2,1,0:T(8,128)} %rev.16, f32[8,64,1024]{2,1,0:T(8,128)} %get-tuple-element.241, f32[8,64,1024]{2,1,0:T(8,128)S(1)} %copy-done, f32[8]{0:T(128)S(1)} %bitcast.80, f32[8,64,1024]{2,1,0:T(8,128)} %get-tuple-element.224, ...), kind=kLoop, calls=%fused_computation.14.clone.1 | loop fusion | flops 3670016 | bytes 12582945 | tf_op jit(solution)/shard_map/while/body/eval_jaxpr/add | solution.py:84
  404.3 5.4 fusion.56
  413.0 6.1 %fusion.57 = f32[8,64,1024]{2,1,0:T(8,128)} fusion(f32[8,64,1024]{2,1,0:T(8,128)} %get-tuple-element.242, f32[4,2,64,1024]{3,2,1,0:T(8,128)} %rev.16, f32[8,64,1024]{2,1,0:T(8,128)} %get-tuple-element.241, f32[8,64,1024]{2,1,0:T(8,128)S(1)} %copy-done, f32[8]{0:T(128)S(1)} %bitcast.80, f32[8,64,1024]{2,1,0:T(8,128)} %get-tuple-element.224, ...), kind=kLoop, calls=%fused_computation.14.clone.1 | loop fusion | flops 3670016 | bytes 12582945 | tf_op jit(solution)/shard_map/while/body/eval_jaxpr/add | solution.py:84
  437.9 6.1 %fusion.57 = f32[8,64,1024]{2,1,0:T(8,128)} fusion(f32[8,64,1024]{2,1,0:T(8,128)} %get-tuple-element.242, f32[4,2,64,1024]{3,2,1,0:T(8,128)} %rev.16, f32[8,64,1024]{2,1,0:T(8,128)} %get-tuple-element.241, f32[8,64,1024]{2,1,0:T(8,128)S(1)} %copy-done, f32[8]{0:T(128)S(1)} %bitcast.80, f32[8,64,1024]{2,1,0:T(8,128)} %get-tuple-element.224, ...), kind=kLoop, calls=%fused_computation.14.clone.1 | loop fusion | flops 3670016 | bytes 12582945 | tf_op jit(solution)/shard_map/while/body/eval_jaxpr/add | solution.py:84
  462.8 6.1 %fusion.57 = f32[8,64,1024]{2,1,0:T(8,128)} fusion(f32[8,64,1024]{2,1,0:T(8,128)} %get-tuple-element.242, f32[4,2,64,1024]{3,2,1,0:T(8,128)} %rev.16, f32[8,64,1024]{2,1,0:T(8,128)} %get-tuple-element.241, f32[8,64,1024]{2,1,0:T(8,128)S(1)} %copy-done, f32[8]{0:T(128)S(1)} %bitcast.80, f32[8,64,1024]{2,1,0:T(8,128)} %get-tuple-element.224, ...), kind=kLoop, calls=%fused_computation.14.clone.1 | loop fusion | flops 3670016 | bytes 12582945 | tf_op jit(solution)/shard_map/while/body/eval_jaxpr/add | solution.py:84
  476.8 26.3 %all-to-all-done.2 = f32[8,64,1024]{2,0,1:T(8,128)S(1)} async-done(((f32[8,64,1024]{2,0,1:T(8,128)}), f32[8,64,1024]{2,0,1:T(8,128)S(1)}, u32[]{:S(2)}, u32[]{:S(2)}) %all-to-all-start.2) | async-done | bytes 2097184 | tf_op jit(solution)/shard_map/all_to_all | solution.py:115
  513.3 25.4 %all-to-all-done.3 = f32[64,8,1024]{2,1,0:T(8,128)} async-done(((f32[64,8,1024]{2,1,0:T(8,128)}), f32[64,8,1024]{2,1,0:T(8,128)}, u32[]{:S(2)}, u32[]{:S(2)}) %all-to-all-start.3) | async-done | bytes 2097184 | tf_op jit(solution)/shard_map/all_to_all | solution.py:118
  551.9 6.8 %multiply_reduce_fusion.1 = (f32[]{:T(128)}, f32[]{:T(128)}) fusion(f32[8,64,1024]{2,1,0:T(8,128)S(1)} %copy-done.2, f32[8,64,1024]{2,0,1:T(8,128)S(1)} %bitcast_divide_fusion, f32[8,64,1024]{2,1,0:T(8,128)S(1)} %copy-done.4, f32[8,64,1]{2,0,1:T(8,128)S(1)} %get-tuple-element.131, f32[8,64,1023]{2,0,1:T(8,128)S(1)} %get-tuple-element.129, ...), kind=kLoop, calls=%fused_computation.41 | loop fusion | flops 12582910 | bytes 12910600 | tf_op jit(solution)/shard_map/reduce_sum | solution.py:135
  558.7 37.1 %all-reduce = (f32[]{:T(128)}, f32[]{:T(128)}, f32[]{:T(128)}) all-reduce(f32[]{:T(128)} %get-tuple-element.101, f32[]{:T(128)} %get-tuple-element.100, f32[]{:T(128)} %multiply_reduce_fusion), channel_id=1, replica_groups=mesh['tm'=8,'space'=4] {'tm','space'}, use_global_device_ids=true, to_apply=%region_3.4 | all-reduce | flops 3 | bytes 24 | tf_op jit(solution)/shard_map/psum | solution.py:134
  (267 shorter events, 313.2 us)
Async XLA Ops:
  4.9 31.8 %all-to-all-start = ((f32[8,64,1024]{2,0,1:T(8,128)}), f32[8,64,1024]{2,0,1:T(8,128)S(1)}, u32[]{:S(2)}, u32[]{:S(2)}) async-start(f32[8,64,1024]{2,0,1:T(8,128)} %copy_multiply_fusion), calls=%async_computation | async-start | bytes 4194304 | tf_op jit(solution)/shard_map/all_to_all | solution.py:107
  41.2 30.3 %all-to-all-start.1 = ((f32[64,8,1024]{2,1,0:T(8,128)}), f32[64,8,1024]{2,1,0:T(8,128)S(1)}, u32[]{:S(2)}, u32[]{:S(2)}) async-start(f32[64,8,1024]{2,1,0:T(8,128)} %copy.72), calls=%async_computation.1 | async-start | bytes 4194304 | tf_op jit(solution)/shard_map/all_to_all | solution.py:110
  73.2 8.2 %collective-permute-start = (f32[8,1,1024]{2,1,0:T(1,128)S(1)}, f32[8,1,1024]{2,1,0:T(1,128)S(1)}, u32[]{:S(2)}, u32[]{:S(2)}) collective-permute-start(f32[8,1,1024]{2,1,0:T(1,128)S(1)} %get-tuple-element.206), channel_id=1, source_target_pairs={{0,1},{1,2},{2,3},{3,0},{4,5},{5,6},{6,7},{7,4},{8,9},{9,10},{10,1... | collective-permute-start | bytes 98312 | tf_op jit(solution)/shard_map/while/body/eval_jaxpr/ppermute | solution.py:22
  97.5 8.2 %collective-permute-start = (f32[8,1,1024]{2,1,0:T(1,128)S(1)}, f32[8,1,1024]{2,1,0:T(1,128)S(1)}, u32[]{:S(2)}, u32[]{:S(2)}) collective-permute-start(f32[8,1,1024]{2,1,0:T(1,128)S(1)} %get-tuple-element.206), channel_id=1, source_target_pairs={{0,1},{1,2},{2,3},{3,0},{4,5},{5,6},{6,7},{7,4},{8,9},{9,10},{10,1... | collective-permute-start | bytes 98312 | tf_op jit(solution)/shard_map/while/body/eval_jaxpr/ppermute | solution.py:22
  97.5 8.2 %collective-permute-start.1 = (f32[8,1,1024]{2,1,0:T(1,128)S(1)}, f32[8,1,1024]{2,1,0:T(1,128)S(1)}, u32[]{:S(2)}, u32[]{:S(2)}) collective-permute-start(f32[8,1,1024]{2,1,0:T(1,128)S(1)} %get-tuple-element.207), channel_id=1, source_target_pairs={{1,0},{2,1},{3,2},{0,3},{5,4},{6,5},{7,6},{4,7},{9,8},{10,9},{11,1... | collective-permute-start | bytes 98312 | tf_op jit(solution)/shard_map/while/body/eval_jaxpr/ppermute | solution.py:25
  122.3 8.2 %collective-permute-start = (f32[8,1,1024]{2,1,0:T(1,128)S(1)}, f32[8,1,1024]{2,1,0:T(1,128)S(1)}, u32[]{:S(2)}, u32[]{:S(2)}) collective-permute-start(f32[8,1,1024]{2,1,0:T(1,128)S(1)} %get-tuple-element.206), channel_id=1, source_target_pairs={{0,1},{1,2},{2,3},{3,0},{4,5},{5,6},{6,7},{7,4},{8,9},{9,10},{10,1... | collective-permute-start | bytes 98312 | tf_op jit(solution)/shard_map/while/body/eval_jaxpr/ppermute | solution.py:22
  122.4 8.2 %collective-permute-start.1 = (f32[8,1,1024]{2,1,0:T(1,128)S(1)}, f32[8,1,1024]{2,1,0:T(1,128)S(1)}, u32[]{:S(2)}, u32[]{:S(2)}) collective-permute-start(f32[8,1,1024]{2,1,0:T(1,128)S(1)} %get-tuple-element.207), channel_id=1, source_target_pairs={{1,0},{2,1},{3,2},{0,3},{5,4},{6,5},{7,6},{4,7},{9,8},{10,9},{11,1... | collective-permute-start | bytes 98312 | tf_op jit(solution)/shard_map/while/body/eval_jaxpr/ppermute | solution.py:25
  147.2 8.2 %collective-permute-start = (f32[8,1,1024]{2,1,0:T(1,128)S(1)}, f32[8,1,1024]{2,1,0:T(1,128)S(1)}, u32[]{:S(2)}, u32[]{:S(2)}) collective-permute-start(f32[8,1,1024]{2,1,0:T(1,128)S(1)} %get-tuple-element.206), channel_id=1, source_target_pairs={{0,1},{1,2},{2,3},{3,0},{4,5},{5,6},{6,7},{7,4},{8,9},{9,10},{10,1... | collective-permute-start | bytes 98312 | tf_op jit(solution)/shard_map/while/body/eval_jaxpr/ppermute | solution.py:22
  147.3 8.2 %collective-permute-start.1 = (f32[8,1,1024]{2,1,0:T(1,128)S(1)}, f32[8,1,1024]{2,1,0:T(1,128)S(1)}, u32[]{:S(2)}, u32[]{:S(2)}) collective-permute-start(f32[8,1,1024]{2,1,0:T(1,128)S(1)} %get-tuple-element.207), channel_id=1, source_target_pairs={{1,0},{2,1},{3,2},{0,3},{5,4},{6,5},{7,6},{4,7},{9,8},{10,9},{11,1... | collective-permute-start | bytes 98312 | tf_op jit(solution)/shard_map/while/body/eval_jaxpr/ppermute | solution.py:25
  172.1 8.2 %collective-permute-start = (f32[8,1,1024]{2,1,0:T(1,128)S(1)}, f32[8,1,1024]{2,1,0:T(1,128)S(1)}, u32[]{:S(2)}, u32[]{:S(2)}) collective-permute-start(f32[8,1,1024]{2,1,0:T(1,128)S(1)} %get-tuple-element.206), channel_id=1, source_target_pairs={{0,1},{1,2},{2,3},{3,0},{4,5},{5,6},{6,7},{7,4},{8,9},{9,10},{10,1... | collective-permute-start | bytes 98312 | tf_op jit(solution)/shard_map/while/body/eval_jaxpr/ppermute | solution.py:22
  172.2 8.2 %collective-permute-start.1 = (f32[8,1,1024]{2,1,0:T(1,128)S(1)}, f32[8,1,1024]{2,1,0:T(1,128)S(1)}, u32[]{:S(2)}, u32[]{:S(2)}) collective-permute-start(f32[8,1,1024]{2,1,0:T(1,128)S(1)} %get-tuple-element.207), channel_id=1, source_target_pairs={{1,0},{2,1},{3,2},{0,3},{5,4},{6,5},{7,6},{4,7},{9,8},{10,9},{11,1... | collective-permute-start | bytes 98312 | tf_op jit(solution)/shard_map/while/body/eval_jaxpr/ppermute | solution.py:25
  197.0 8.2 %collective-permute-start = (f32[8,1,1024]{2,1,0:T(1,128)S(1)}, f32[8,1,1024]{2,1,0:T(1,128)S(1)}, u32[]{:S(2)}, u32[]{:S(2)}) collective-permute-start(f32[8,1,1024]{2,1,0:T(1,128)S(1)} %get-tuple-element.206), channel_id=1, source_target_pairs={{0,1},{1,2},{2,3},{3,0},{4,5},{5,6},{6,7},{7,4},{8,9},{9,10},{10,1... | collective-permute-start | bytes 98312 | tf_op jit(solution)/shard_map/while/body/eval_jaxpr/ppermute | solution.py:22
  197.0 8.2 %collective-permute-start.1 = (f32[8,1,1024]{2,1,0:T(1,128)S(1)}, f32[8,1,1024]{2,1,0:T(1,128)S(1)}, u32[]{:S(2)}, u32[]{:S(2)}) collective-permute-start(f32[8,1,1024]{2,1,0:T(1,128)S(1)} %get-tuple-element.207), channel_id=1, source_target_pairs={{1,0},{2,1},{3,2},{0,3},{5,4},{6,5},{7,6},{4,7},{9,8},{10,9},{11,1... | collective-permute-start | bytes 98312 | tf_op jit(solution)/shard_map/while/body/eval_jaxpr/ppermute | solution.py:25
  221.9 8.2 %collective-permute-start = (f32[8,1,1024]{2,1,0:T(1,128)S(1)}, f32[8,1,1024]{2,1,0:T(1,128)S(1)}, u32[]{:S(2)}, u32[]{:S(2)}) collective-permute-start(f32[8,1,1024]{2,1,0:T(1,128)S(1)} %get-tuple-element.206), channel_id=1, source_target_pairs={{0,1},{1,2},{2,3},{3,0},{4,5},{5,6},{6,7},{7,4},{8,9},{9,10},{10,1... | collective-permute-start | bytes 98312 | tf_op jit(solution)/shard_map/while/body/eval_jaxpr/ppermute | solution.py:22
  221.9 8.2 %collective-permute-start.1 = (f32[8,1,1024]{2,1,0:T(1,128)S(1)}, f32[8,1,1024]{2,1,0:T(1,128)S(1)}, u32[]{:S(2)}, u32[]{:S(2)}) collective-permute-start(f32[8,1,1024]{2,1,0:T(1,128)S(1)} %get-tuple-element.207), channel_id=1, source_target_pairs={{1,0},{2,1},{3,2},{0,3},{5,4},{6,5},{7,6},{4,7},{9,8},{10,9},{11,1... | collective-permute-start | bytes 98312 | tf_op jit(solution)/shard_map/while/body/eval_jaxpr/ppermute | solution.py:25
  246.7 8.2 %collective-permute-start = (f32[8,1,1024]{2,1,0:T(1,128)S(1)}, f32[8,1,1024]{2,1,0:T(1,128)S(1)}, u32[]{:S(2)}, u32[]{:S(2)}) collective-permute-start(f32[8,1,1024]{2,1,0:T(1,128)S(1)} %get-tuple-element.206), channel_id=1, source_target_pairs={{0,1},{1,2},{2,3},{3,0},{4,5},{5,6},{6,7},{7,4},{8,9},{9,10},{10,1... | collective-permute-start | bytes 98312 | tf_op jit(solution)/shard_map/while/body/eval_jaxpr/ppermute | solution.py:22
  246.8 8.2 %collective-permute-start.1 = (f32[8,1,1024]{2,1,0:T(1,128)S(1)}, f32[8,1,1024]{2,1,0:T(1,128)S(1)}, u32[]{:S(2)}, u32[]{:S(2)}) collective-permute-start(f32[8,1,1024]{2,1,0:T(1,128)S(1)} %get-tuple-element.207), channel_id=1, source_target_pairs={{1,0},{2,1},{3,2},{0,3},{5,4},{6,5},{7,6},{4,7},{9,8},{10,9},{11,1... | collective-permute-start | bytes 98312 | tf_op jit(solution)/shard_map/while/body/eval_jaxpr/ppermute | solution.py:25
  271.6 8.2 %collective-permute-start = (f32[8,1,1024]{2,1,0:T(1,128)S(1)}, f32[8,1,1024]{2,1,0:T(1,128)S(1)}, u32[]{:S(2)}, u32[]{:S(2)}) collective-permute-start(f32[8,1,1024]{2,1,0:T(1,128)S(1)} %get-tuple-element.206), channel_id=1, source_target_pairs={{0,1},{1,2},{2,3},{3,0},{4,5},{5,6},{6,7},{7,4},{8,9},{9,10},{10,1... | collective-permute-start | bytes 98312 | tf_op jit(solution)/shard_map/while/body/eval_jaxpr/ppermute | solution.py:22
  271.7 8.2 %collective-permute-start.1 = (f32[8,1,1024]{2,1,0:T(1,128)S(1)}, f32[8,1,1024]{2,1,0:T(1,128)S(1)}, u32[]{:S(2)}, u32[]{:S(2)}) collective-permute-start(f32[8,1,1024]{2,1,0:T(1,128)S(1)} %get-tuple-element.207), channel_id=1, source_target_pairs={{1,0},{2,1},{3,2},{0,3},{5,4},{6,5},{7,6},{4,7},{9,8},{10,9},{11,1... | collective-permute-start | bytes 98312 | tf_op jit(solution)/shard_map/while/body/eval_jaxpr/ppermute | solution.py:25
  296.5 8.2 %collective-permute-start = (f32[8,1,1024]{2,1,0:T(1,128)S(1)}, f32[8,1,1024]{2,1,0:T(1,128)S(1)}, u32[]{:S(2)}, u32[]{:S(2)}) collective-permute-start(f32[8,1,1024]{2,1,0:T(1,128)S(1)} %get-tuple-element.206), channel_id=1, source_target_pairs={{0,1},{1,2},{2,3},{3,0},{4,5},{5,6},{6,7},{7,4},{8,9},{9,10},{10,1... | collective-permute-start | bytes 98312 | tf_op jit(solution)/shard_map/while/body/eval_jaxpr/ppermute | solution.py:22
  296.6 8.2 %collective-permute-start.1 = (f32[8,1,1024]{2,1,0:T(1,128)S(1)}, f32[8,1,1024]{2,1,0:T(1,128)S(1)}, u32[]{:S(2)}, u32[]{:S(2)}) collective-permute-start(f32[8,1,1024]{2,1,0:T(1,128)S(1)} %get-tuple-element.207), channel_id=1, source_target_pairs={{1,0},{2,1},{3,2},{0,3},{5,4},{6,5},{7,6},{4,7},{9,8},{10,9},{11,1... | collective-permute-start | bytes 98312 | tf_op jit(solution)/shard_map/while/body/eval_jaxpr/ppermute | solution.py:25
  321.4 8.2 %collective-permute-start = (f32[8,1,1024]{2,1,0:T(1,128)S(1)}, f32[8,1,1024]{2,1,0:T(1,128)S(1)}, u32[]{:S(2)}, u32[]{:S(2)}) collective-permute-start(f32[8,1,1024]{2,1,0:T(1,128)S(1)} %get-tuple-element.206), channel_id=1, source_target_pairs={{0,1},{1,2},{2,3},{3,0},{4,5},{5,6},{6,7},{7,4},{8,9},{9,10},{10,1... | collective-permute-start | bytes 98312 | tf_op jit(solution)/shard_map/while/body/eval_jaxpr/ppermute | solution.py:22
  321.4 8.2 %collective-permute-start.1 = (f32[8,1,1024]{2,1,0:T(1,128)S(1)}, f32[8,1,1024]{2,1,0:T(1,128)S(1)}, u32[]{:S(2)}, u32[]{:S(2)}) collective-permute-start(f32[8,1,1024]{2,1,0:T(1,128)S(1)} %get-tuple-element.207), channel_id=1, source_target_pairs={{1,0},{2,1},{3,2},{0,3},{5,4},{6,5},{7,6},{4,7},{9,8},{10,9},{11,1... | collective-permute-start | bytes 98312 | tf_op jit(solution)/shard_map/while/body/eval_jaxpr/ppermute | solution.py:25
  346.3 8.2 %collective-permute-start = (f32[8,1,1024]{2,1,0:T(1,128)S(1)}, f32[8,1,1024]{2,1,0:T(1,128)S(1)}, u32[]{:S(2)}, u32[]{:S(2)}) collective-permute-start(f32[8,1,1024]{2,1,0:T(1,128)S(1)} %get-tuple-element.206), channel_id=1, source_target_pairs={{0,1},{1,2},{2,3},{3,0},{4,5},{5,6},{6,7},{7,4},{8,9},{9,10},{10,1... | collective-permute-start | bytes 98312 | tf_op jit(solution)/shard_map/while/body/eval_jaxpr/ppermute | solution.py:22
  346.3 8.2 %collective-permute-start.1 = (f32[8,1,1024]{2,1,0:T(1,128)S(1)}, f32[8,1,1024]{2,1,0:T(1,128)S(1)}, u32[]{:S(2)}, u32[]{:S(2)}) collective-permute-start(f32[8,1,1024]{2,1,0:T(1,128)S(1)} %get-tuple-element.207), channel_id=1, source_target_pairs={{1,0},{2,1},{3,2},{0,3},{5,4},{6,5},{7,6},{4,7},{9,8},{10,9},{11,1... | collective-permute-start | bytes 98312 | tf_op jit(solution)/shard_map/while/body/eval_jaxpr/ppermute | solution.py:25
  371.1 8.2 %collective-permute-start = (f32[8,1,1024]{2,1,0:T(1,128)S(1)}, f32[8,1,1024]{2,1,0:T(1,128)S(1)}, u32[]{:S(2)}, u32[]{:S(2)}) collective-permute-start(f32[8,1,1024]{2,1,0:T(1,128)S(1)} %get-tuple-element.206), channel_id=1, source_target_pairs={{0,1},{1,2},{2,3},{3,0},{4,5},{5,6},{6,7},{7,4},{8,9},{9,10},{10,1... | collective-permute-start | bytes 98312 | tf_op jit(solution)/shard_map/while/body/eval_jaxpr/ppermute | solution.py:22
  371.2 8.2 %collective-permute-start.1 = (f32[8,1,1024]{2,1,0:T(1,128)S(1)}, f32[8,1,1024]{2,1,0:T(1,128)S(1)}, u32[]{:S(2)}, u32[]{:S(2)}) collective-permute-start(f32[8,1,1024]{2,1,0:T(1,128)S(1)} %get-tuple-element.207), channel_id=1, source_target_pairs={{1,0},{2,1},{3,2},{0,3},{5,4},{6,5},{7,6},{4,7},{9,8},{10,9},{11,1... | collective-permute-start | bytes 98312 | tf_op jit(solution)/shard_map/while/body/eval_jaxpr/ppermute | solution.py:25
  396.0 8.2 %collective-permute-start = (f32[8,1,1024]{2,1,0:T(1,128)S(1)}, f32[8,1,1024]{2,1,0:T(1,128)S(1)}, u32[]{:S(2)}, u32[]{:S(2)}) collective-permute-start(f32[8,1,1024]{2,1,0:T(1,128)S(1)} %get-tuple-element.206), channel_id=1, source_target_pairs={{0,1},{1,2},{2,3},{3,0},{4,5},{5,6},{6,7},{7,4},{8,9},{9,10},{10,1... | collective-permute-start | bytes 98312 | tf_op jit(solution)/shard_map/while/body/eval_jaxpr/ppermute | solution.py:22
  420.9 8.2 %collective-permute-start = (f32[8,1,1024]{2,1,0:T(1,128)S(1)}, f32[8,1,1024]{2,1,0:T(1,128)S(1)}, u32[]{:S(2)}, u32[]{:S(2)}) collective-permute-start(f32[8,1,1024]{2,1,0:T(1,128)S(1)} %get-tuple-element.206), channel_id=1, source_target_pairs={{0,1},{1,2},{2,3},{3,0},{4,5},{5,6},{6,7},{7,4},{8,9},{9,10},{10,1... | collective-permute-start | bytes 98312 | tf_op jit(solution)/shard_map/while/body/eval_jaxpr/ppermute | solution.py:22
  445.8 8.2 %collective-permute-start = (f32[8,1,1024]{2,1,0:T(1,128)S(1)}, f32[8,1,1024]{2,1,0:T(1,128)S(1)}, u32[]{:S(2)}, u32[]{:S(2)}) collective-permute-start(f32[8,1,1024]{2,1,0:T(1,128)S(1)} %get-tuple-element.206), channel_id=1, source_target_pairs={{0,1},{1,2},{2,3},{3,0},{4,5},{5,6},{6,7},{7,4},{8,9},{9,10},{10,1... | collective-permute-start | bytes 98312 | tf_op jit(solution)/shard_map/while/body/eval_jaxpr/ppermute | solution.py:22
  473.0 30.2 %all-to-all-start.2 = ((f32[8,64,1024]{2,0,1:T(8,128)}), f32[8,64,1024]{2,0,1:T(8,128)S(1)}, u32[]{:S(2)}, u32[]{:S(2)}) async-start(f32[8,64,1024]{2,0,1:T(8,128)} %copy.74), calls=%async_computation.2 | async-start | bytes 4194304 | tf_op jit(solution)/shard_map/all_to_all | solution.py:115
  507.7 31.1 %all-to-all-start.3 = ((f32[64,8,1024]{2,1,0:T(8,128)}), f32[64,8,1024]{2,1,0:T(8,128)}, u32[]{:S(2)}, u32[]{:S(2)}) async-start(f32[64,8,1024]{2,1,0:T(8,128)} %copy.77), calls=%async_computation.3 | async-start | bytes 4194304 | tf_op jit(solution)/shard_map/all_to_all | solution.py:118
  (28 other events, 131.3 us)
where the time goes:
time: 607 us; the launch traced here: 605 us
  other arithmetic  227 us (37%)
  local copies, waits for them, and re-layouts  146 us (24%)
  waiting for transfers between devices  100 us (16%)
  starting transfers between devices  82.6 us (14%)
  blocking collectives  37.1 us (6%)
  between operations  7.31 us (1%)
    add x16, other arithmetic, one_sweep(): values + damping * (partner_diag * defect - signed_col * partner(defect))...  96.5 us
    sub x16, other arithmetic, one_sweep(): defect = spectrum - applied  85.9 us
    rev x33, local copies, waits for them, and re-layouts, partner(): jnp.flip(values.reshape(extent[0] // 2, 2, extent[1], extent[2]), axis=1)  80.9 us
    ppermute x17, starting transfers between devices, padded_2(): lax.ppermute(lax.slice_in_dim(block, 0, width, axis=dim), axis, backward)  60.8 us
    slice x34, local copies, waits for them, and re-layouts, neg_laplace(): jnp.roll(middle, -1, axis=2)  46.9 us
    psum x1, blocking collectives, on_device(): lax.psum((jnp.sum(residual * residual), jnp.sum(residual * applied), jnp....  37.1 us
    while x16, other arithmetic  26.4 us
    all_to_all x1, waiting for transfers between devices, precondition(): lax.all_to_all(solved, 'tm', split_axis=1, concat_axis=0, tiled=True)  26.3 us
  transfers between devices with their start and end apart: 39, of which 6 were waited for; matrix products, arithmetic and copies ran while one was open for 13% of the time, Pallas kernels for 0%

commit v1 on v0

--- a/solution.py
+++ b/solution.py
@@ -1,6 +1,9 @@
+import functools
 import jax
 import jax.numpy as jnp
 from jax import lax
+from jax.experimental import pallas as pl
+from jax.experimental.pallas import tpu as pltpu
 from jax.sharding import PartitionSpec as P
 
 NT = 64
@@ -61,35 +64,148 @@
     return 4.0 * values - neighbours
 
 
-def partner(values):
-    extent = values.shape
-    return jnp.flip(values.reshape(extent[0] // 2, 2, extent[1], extent[2]), axis=1).reshape(extent)
-
-
-def make_sweep(spectrum, shifts, signed, frozen, mobility, laplace_fn):
-    shift_col = shifts[:, None, None]
-    signed_col = signed[:, None, None]
-    diagonal = shift_col + (frozen + 4.0 * mobility)[None]
-    partner_diag = partner(diagonal)
-    denominator = diagonal * partner_diag + signed_col * signed_col
-
-    def one_sweep(sweep_id, values):
-        applied = (
-            (shift_col + frozen[None]) * values
-            + mobility[None] * laplace_fn(values)
-            + signed_col * partner(values)
+TILE = 8
+
+
+def relax_kernel(
+    count, shift_ref, signed_ref, spec_ref, base_ref, mob_ref, out_ref,
+    state, gain, cross, start_val, sent, halo, send_sem, recv_sem,
+):
+    coefs, rows, cols = spec_ref.shape
+    pairs, tiles = coefs // 2, rows // TILE
+    keep = 1.0 - damping
+    me = lax.axis_index("space")
+    prev, after = lax.rem(me + count - 1, count), lax.rem(me + 1, count)
+
+    barrier = pltpu.get_barrier_semaphore()
+    for other in (prev, after):
+        pl.semaphore_signal(
+            barrier, inc=1, device_id={"space": other}, device_id_type=pl.DeviceIdType.MESH
         )
-        defect = spectrum - applied
-        return (
-            values + damping * (partner_diag * defect - signed_col * partner(defect)) / denominator
+    pl.semaphore_wait(barrier, 2)
+
+    def edge(slot, q, side):
+        return pltpu.make_async_remote_copy(
+            src_ref=sent.at[slot, q, side],
+            dst_ref=halo.at[slot, q, 1 - side],
+            send_sem=send_sem.at[slot, q, side],
+            recv_sem=recv_sem.at[slot, q, 1 - side],
+            device_id={"space": prev if side == 0 else after},
+            device_id_type=pl.DeviceIdType.MESH,
         )
 
-    return one_sweep
+    def send(slot, q):
+        for side in range(2):
+            edge(slot, q, side).start()
+
+    def prepare(q, _):
+        sig_e, sig_o = shift_ref[2 * q], shift_ref[2 * q + 1]
+        c_e = signed_ref[2 * q]
+        for t in [0, tiles - 1] + list(range(1, tiles - 1)):
+            span = pl.ds(t * TILE, TILE)
+            mob, base = mob_ref[span, :], base_ref[span, :]
+            d_e, d_o = sig_e + base, sig_o + base
+            scale = damping / (d_e * d_o + c_e * c_e)
+            s_e, s_o = spec_ref[2 * q, span, :], spec_ref[2 * q + 1, span, :]
+            b_e = scale * (d_o * s_e - c_e * s_o)
+            b_o = scale * (d_e * s_o + c_e * s_e)
+            scaled = scale * mob
+            gain[2 * q, span, :] = scaled * d_o
+            gain[2 * q + 1, span, :] = scaled * d_e
+            cross[q, span, :] = scaled * c_e
+            start_val[2 * q, span, :] = b_e
+            start_val[2 * q + 1, span, :] = b_o
+            own = pl.ds((t + 1) * TILE, TILE)
+            state[0, 2 * q, own, :] = b_e
+            state[0, 2 * q + 1, own, :] = b_o
+            if t == 0:
+                sent[0, q, 0, 0:1, :] = b_e[0:1]
+                sent[0, q, 0, 1:2, :] = b_o[0:1]
+            if t == tiles - 1:
+                sent[0, q, 1, 0:1, :] = b_e[TILE - 1 :]
+                sent[0, q, 1, 1:2, :] = b_o[TILE - 1 :]
+                send(0, q)
+        return 0
+
+    lax.fori_loop(0, pairs, prepare, 0)
+
+    def around(slot, m, t):
+        top = (t + 1) * TILE
+        mid = state[slot, m, pl.ds(top, TILE), :]
+        total = state[slot, m, pl.ds(top - 1, TILE), :] + state[slot, m, pl.ds(top + 1, TILE), :]
+        total = total + (pltpu.roll(mid, 1, 1) + pltpu.roll(mid, cols - 1, 1))
+        return mid, total
+
+    def sweep(s, _):
+        now = lax.rem(s, 2)
+        later = 1 - now
+
+        def one_pair(q, _):
+            for side in range(2):
+                edge(now, q, side).wait()
+            for part in range(2):
+                state[now, 2 * q + part, pl.ds(TILE - 1, 1), :] = halo[now, q, 0, part : part + 1, :]
+                state[now, 2 * q + part, pl.ds(TILE + rows, 1), :] = halo[now, q, 1, part : part + 1, :]
+            for t in [0, tiles - 1] + list(range(1, tiles - 1)):
+                span = pl.ds(t * TILE, TILE)
+                own = pl.ds((t + 1) * TILE, TILE)
+                y_e, n_e = around(now, 2 * q, t)
+                y_o, n_o = around(now, 2 * q + 1, t)
+                c = cross[q, span, :]
+                new_e = keep * y_e + start_val[2 * q, span, :] + (gain[2 * q, span, :] * n_e - c * n_o)
+                new_o = keep * y_o + start_val[2 * q + 1, span, :] + (gain[2 * q + 1, span, :] * n_o + c * n_e)
+                state[later, 2 * q, own, :] = new_e
+                state[later, 2 * q + 1, own, :] = new_o
+                if t == 0:
+                    sent[later, q, 0, 0:1, :] = new_e[0:1]
+                    sent[later, q, 0, 1:2, :] = new_o[0:1]
+                if t == tiles - 1:
+                    sent[later, q, 1, 0:1, :] = new_e[TILE - 1 :]
+                    sent[later, q, 1, 1:2, :] = new_o[TILE - 1 :]
+
+                    @pl.when(s < SWEEPS - 2)
+                    def _():
+                        send(later, q)
+
+            return 0
+
+        return lax.fori_loop(0, pairs, one_pair, 0)
+
+    lax.fori_loop(0, SWEEPS - 1, sweep, 0)
+    last = (SWEEPS - 1) % 2
+
+    def store(m, _):
+        out_ref[m] = state[last, m, TILE : TILE + rows, :]
+        return 0
+
+    lax.fori_loop(0, coefs, store, 0)
 
 
 def relax_pairs(spectrum, shifts, signed, frozen, mobility):
-    one_sweep = make_sweep(spectrum, shifts, signed, frozen, mobility, neg_laplace)
-    return lax.fori_loop(0, SWEEPS, one_sweep, jnp.zeros_like(spectrum))
+    coefs, rows, cols = spectrum.shape
+    pairs = coefs // 2
+    count = lax.axis_size("space")
+    vmem = pl.BlockSpec(memory_space=pltpu.VMEM)
+    smem = pl.BlockSpec(memory_space=pltpu.SMEM)
+    return pl.pallas_call(
+        functools.partial(relax_kernel, count),
+        out_shape=jax.ShapeDtypeStruct(spectrum.shape, jnp.float32),
+        in_specs=[smem, smem, vmem, vmem, vmem],
+        out_specs=vmem,
+        scratch_shapes=[
+            pltpu.VMEM((2, coefs, rows + 2 * TILE, cols), jnp.float32),
+            pltpu.VMEM((coefs, rows, cols), jnp.float32),
+            pltpu.VMEM((pairs, rows, cols), jnp.float32),
+            pltpu.VMEM((coefs, rows, cols), jnp.float32),
+            pltpu.VMEM((2, pairs, 2, 2, cols), jnp.float32),
+            pltpu.VMEM((2, pairs, 2, 2, cols), jnp.float32),
+            pltpu.SemaphoreType.DMA((2, pairs, 2)),
+            pltpu.SemaphoreType.DMA((2, pairs, 2)),
+        ],
+        compiler_params=pltpu.CompilerParams(
+            collective_id=0, has_side_effects=True, vmem_limit_bytes=32 * 1024 * 1024
+        ),
+    )(shifts, signed, spectrum, frozen + 4.0 * mobility, mobility)
 
 
 def precondition(values, frozen, mobility, tables):

time: 607 us -> 274 us (0.45)
  other arithmetic: 227 us -> 13.1 us
  local copies, waits for them, and re-layouts: 146 us -> 15.5 us
  Pallas kernels: 0 us -> 66.2 us
  starting transfers between devices: 82.6 us -> 20.7 us
  waiting for transfers between devices: 100 us -> 109 us
    add x19 -> x1, other arithmetic: 102 us -> 0.07 us  [relax_pairs(): frozen + 4.0 * mobility]
    sub x16 -> x0, other arithmetic: 85.9 us -> none  [one_sweep(): defect = spectrum - applied]
    rev x33 -> x0, local copies, waits for them, and re-layouts: 80.9 us -> none  [partner(): jnp.flip(values.reshape(extent[0] // 2, 2, extent[1], extent[2]), axis=1)]
    pallas_call x0 -> x1, Pallas kernels: none -> 66.2 us  [relax_pairs(): pl.pallas_call(functools.partial(relax_kernel, count), out_shape=jax.Shap...]
    ppermute x17 -> x1, starting transfers between devices: 60.8 us -> 2.06 us  [padded_2(): lax.ppermute(lax.slice_in_dim(block, 0, width, axis=dim), axis, backward)]
    slice x34 -> x2, local copies, waits for them, and re-layouts: 46.9 us -> 0.97 us  [neg_laplace(): jnp.roll(middle, -1, axis=2)]
    while x16 -> x0, other arithmetic: 26.4 us -> none
    all_to_all x1, waiting for transfers between devices: 17.4 us -> 25.8 us  [precondition(): lax.all_to_all(spectrum, 'tm', split_axis=0, concat_axis=1, tiled=True)]
  transfers between devices with their start and end apart: 39 -> 7, of which waited for: 6 -> 6; matrix products, arithmetic and copies ran while one was open for 13% -> 1% of each run, Pallas kernels for 0% -> 0%
where the time goes in v1:
time: 274 us; the launch traced here: 273 us
  waiting for transfers between devices  109 us (40%)
  Pallas kernels  66.2 us (24%)
  blocking collectives  37.1 us (14%)
  starting transfers between devices  20.7 us (8%)
  local copies, waits for them, and re-layouts  15.5 us (6%)
  other arithmetic  13.1 us (5%)
  between operations  7.1 us (3%)
  matrix products  3.9 us (1%)
    pallas_call x1, Pallas kernels, relax_pairs(): pl.pallas_call(functools.partial(relax_kernel, count), out_shape=jax.Shap...  66.2 us
    psum x1, blocking collectives, on_device(): lax.psum((jnp.sum(residual * residual), jnp.sum(residual * applied), jnp....  37.1 us
    all_to_all x1, waiting for transfers between devices, precondition(): lax.all_to_all(solved, 'tm', split_axis=1, concat_axis=0, tiled=True)  26.5 us
    all_to_all x1, waiting for transfers between devices, precondition(): lax.all_to_all(weighted, 'tm', split_axis=1, concat_axis=0, tiled=True)  26.3 us
    all_to_all x1, waiting for transfers between devices, precondition(): lax.all_to_all(spectrum, 'tm', split_axis=0, concat_axis=1, tiled=True)  25.8 us
    all_to_all x1, waiting for transfers between devices, precondition(): lax.all_to_all(in_time, 'tm', split_axis=0, concat_axis=1, tiled=True)  25.3 us
    reduce_sum x1, other arithmetic, on_device(): jnp.sum(applied * applied)  6.76 us
  transfers between devices with their start and end apart: 7, of which 6 were waited for; matrix products, arithmetic and copies ran while one was open for 1% of the time, Pallas kernels for 0%

profile of v1, /device:TPU:0, one launch (start us, length us, event | category | flops | bytes accessed | tf_op | source)
XLA Modules:
  0.0 273.1 jit_solution(2064471242135720479)
XLA Ops:
  0.7 4.1 %copy_multiply_fusion = f32[8,64,1024]{2,0,1:T(8,128)} fusion(f32[8,64,1024]{2,1,0:T(8,128)} %param.8, f32[8]{0:T(128)S(1)} %dynamic_slice.11), kind=kLoop, calls=%fused_computation.26 | loop fusion | flops 524288 | bytes 4194336 | tf_op jit(solution)/shard_map/mul | solution.py:219
  4.9 5.2 %all-to-all-start = ((f32[8,64,1024]{2,0,1:T(8,128)}), f32[8,64,1024]{2,0,1:T(8,128)S(1)}, u32[]{:S(2)}, u32[]{:S(2)}) async-start(f32[8,64,1024]{2,0,1:T(8,128)} %copy_multiply_fusion), calls=%async_computation | async-start | bytes 4194304 | tf_op jit(solution)/shard_map/all_to_all | solution.py:223
  10.1 0.1 multiply_cosine_fusion
  10.4 26.3 %all-to-all-done = f32[8,64,1024]{2,0,1:T(8,128)S(1)} async-done(((f32[8,64,1024]{2,0,1:T(8,128)}), f32[8,64,1024]{2,0,1:T(8,128)S(1)}, u32[]{:S(2)}, u32[]{:S(2)}) %all-to-all-start) | async-done | bytes 2097184 | tf_op jit(solution)/shard_map/all_to_all | solution.py:223
  36.7 1.9 fusion.13
  38.6 2.5 copy.72
  41.2 3.7 %all-to-all-start.1 = ((f32[64,8,1024]{2,1,0:T(8,128)}), f32[64,8,1024]{2,1,0:T(8,128)S(1)}, u32[]{:S(2)}, u32[]{:S(2)}) async-start(f32[64,8,1024]{2,1,0:T(8,128)} %copy.72), calls=%async_computation.1 | async-start | bytes 4194304 | tf_op jit(solution)/shard_map/all_to_all | solution.py:226
  45.7 25.8 %all-to-all-done.1 = f32[64,8,1024]{2,1,0:T(8,128)S(1)} async-done(((f32[64,8,1024]{2,1,0:T(8,128)}), f32[64,8,1024]{2,1,0:T(8,128)S(1)}, u32[]{:S(2)}, u32[]{:S(2)}) %all-to-all-start.1) | async-done | bytes 2097184 | tf_op jit(solution)/shard_map/all_to_all | solution.py:226
  71.4 0.2 copy.99
  71.7 66.2 %shard_map.59 = f32[8,64,1024]{2,1,0:T(8,128)S(1)} custom-call(f32[8]{0:T(128)S(1)} %dynamic_slice.9.shift_ref, f32[8]{0:T(128)S(1)} %dynamic_slice.10.signed_ref, f32[8,64,1024]{2,1,0:T(8,128)S(1)} %bitcast.34, f32[64,1024]{1,0:T(8,128)S(1)} %fusion.20.base_ref, f32[64,1024]{1,0:T(8,128)S(1)} %copy-done), custom_call_target="tpu_custom_call" | custom-call | tf_op jit(solution)/shard_map/pallas_call | solution.py:190
  137.9 2.5 copy.74
  140.4 3.6 %all-to-all-start.2 = ((f32[8,64,1024]{2,0,1:T(8,128)}), f32[8,64,1024]{2,0,1:T(8,128)S(1)}, u32[]{:S(2)}, u32[]{:S(2)}) async-start(f32[8,64,1024]{2,0,1:T(8,128)} %copy.74), calls=%async_computation.2 | async-start | bytes 4194304 | tf_op jit(solution)/shard_map/all_to_all | solution.py:231
  144.1 26.5 %all-to-all-done.2 = f32[8,64,1024]{2,0,1:T(8,128)S(1)} async-done(((f32[8,64,1024]{2,0,1:T(8,128)}), f32[8,64,1024]{2,0,1:T(8,128)S(1)}, u32[]{:S(2)}, u32[]{:S(2)}) %all-to-all-start.2) | async-done | bytes 2097184 | tf_op jit(solution)/shard_map/all_to_all | solution.py:231
  170.6 2.0 fusion.11
  172.6 2.5 copy.77
  175.1 4.7 %all-to-all-start.3 = ((f32[64,8,1024]{2,1,0:T(8,128)}), f32[64,8,1024]{2,1,0:T(8,128)}, u32[]{:S(2)}, u32[]{:S(2)}) async-start(f32[64,8,1024]{2,1,0:T(8,128)} %copy.77), calls=%async_computation.3 | async-start | bytes 4194304 | tf_op jit(solution)/shard_map/all_to_all | solution.py:234
  179.8 1.1 multiply_reduce_fusion
  180.9 25.3 %all-to-all-done.3 = f32[64,8,1024]{2,1,0:T(8,128)} async-done(((f32[64,8,1024]{2,1,0:T(8,128)}), f32[64,8,1024]{2,1,0:T(8,128)}, u32[]{:S(2)}, u32[]{:S(2)}) %all-to-all-start.3) | async-done | bytes 2097184 | tf_op jit(solution)/shard_map/all_to_all | solution.py:234
  206.2 2.8 %copy.78 = f32[8,8,8,1024]{3,1,2,0:T(8,128)S(1)} copy(f32[8,8,8,1024]{3,2,1,0:T(8,128)} %bitcast.13) | data formatting | bytes 4194304 | tf_op jit(solution)/shard_map/all_to_all | solution.py:234
  209.1 0.3 bitcast_divide_fusion
  209.4 0.3 slice.56
  209.7 0.8 fusion.30
  210.6 1.4 collective-permute-start
  212.0 2.1 collective-permute-start.1
  214.1 0.1 fusion.31
  214.3 0.3 copy.80
  214.5 1.6 collective-permute-done.1
  216.1 4.0 %collective-permute-done.2 = f32[8,1,1024]{2,0,1:T(8,128)S(1)} collective-permute-done((f32[8,1,1024]{2,0,1:T(8,128)S(1)}, f32[8,1,1024]{2,0,1:T(8,128)S(1)}, u32[]{:S(2)}, u32[]{:S(2)}) %collective-permute-start.2) | collective-permute-done | bytes 32800 | tf_op jit(solution)/shard_map/ppermute | solution.py:25
  220.1 6.8 %multiply_reduce_fusion.1 = (f32[]{:T(128)}, f32[]{:T(128)}) fusion(f32[8,64,1024]{2,1,0:T(8,128)S(1)} %copy-done.2, f32[8,64,1024]{2,0,1:T(8,128)S(1)} %bitcast_divide_fusion, f32[8,64,1024]{2,1,0:T(8,128)S(1)} %copy-done.3, f32[8,64,1]{2,0,1:T(8,128)S(1)} %get-tuple-element.29, f32[8,64,1023]{2,0,1:T(8,128)S(1)} %get-tuple-element.27, ...), kind=kLoop, calls=%fused_computation.24 | loop fusion | flops 12582910 | bytes 12910600 | tf_op jit(solution)/shard_map/reduce_sum | solution.py:251
  226.9 37.1 %all-reduce = (f32[]{:T(128)}, f32[]{:T(128)}, f32[]{:T(128)}) all-reduce(f32[]{:T(128)} %get-tuple-element.23, f32[]{:T(128)} %get-tuple-element.22, f32[]{:T(128)} %multiply_reduce_fusion), channel_id=1, replica_groups=mesh['tm'=8,'space'=4] {'tm','space'}, use_global_device_ids=true, to_apply=%region_1.2 | all-reduce | flops 3 | bytes 24 | tf_op jit(solution)/shard_map/psum | solution.py:250
  269.1 0.3 broadcast_multiply_fusion
  269.4 2.5 copy.84
  (37 shorter events, 1.1 us)
Async XLA Ops:
  4.9 31.8 %all-to-all-start = ((f32[8,64,1024]{2,0,1:T(8,128)}), f32[8,64,1024]{2,0,1:T(8,128)S(1)}, u32[]{:S(2)}, u32[]{:S(2)}) async-start(f32[8,64,1024]{2,0,1:T(8,128)} %copy_multiply_fusion), calls=%async_computation | async-start | bytes 4194304 | tf_op jit(solution)/shard_map/all_to_all | solution.py:223
  41.1 4.4 %copy-start = (f32[64,1024]{1,0:T(8,128)S(1)}, f32[64,1024]{1,0:T(8,128)}, u32[]{:S(2)}) copy-start(f32[64,1024]{1,0:T(8,128)} %mob_ref.1) | copy-start | bytes 786436
  41.2 4.4 %copy-start.4 = (f32[64,1024]{1,0:T(8,128)S(1)}, f32[64,1024]{1,0:T(8,128)}, u32[]{:S(2)}) copy-start(f32[64,1024]{1,0:T(8,128)} %param.7) | copy-start | bytes 786436
  41.2 30.3 %all-to-all-start.1 = ((f32[64,8,1024]{2,1,0:T(8,128)}), f32[64,8,1024]{2,1,0:T(8,128)S(1)}, u32[]{:S(2)}, u32[]{:S(2)}) async-start(f32[64,8,1024]{2,1,0:T(8,128)} %copy.72), calls=%async_computation.1 | async-start | bytes 4194304 | tf_op jit(solution)/shard_map/all_to_all | solution.py:226
  140.4 30.2 %all-to-all-start.2 = ((f32[8,64,1024]{2,0,1:T(8,128)}), f32[8,64,1024]{2,0,1:T(8,128)S(1)}, u32[]{:S(2)}, u32[]{:S(2)}) async-start(f32[8,64,1024]{2,0,1:T(8,128)} %copy.74), calls=%async_computation.2 | async-start | bytes 4194304 | tf_op jit(solution)/shard_map/all_to_all | solution.py:231
  175.1 4.7 %copy-start.1 = (f32[8,64,1024]{2,1,0:T(8,128)S(1)}, f32[8,64,1024]{2,1,0:T(8,128)}, u32[]{:S(2)}) copy-start(f32[8,64,1024]{2,1,0:T(8,128)} %param.8) | copy-start | bytes 6291460
  175.1 31.1 %all-to-all-start.3 = ((f32[64,8,1024]{2,1,0:T(8,128)}), f32[64,8,1024]{2,1,0:T(8,128)}, u32[]{:S(2)}, u32[]{:S(2)}) async-start(f32[64,8,1024]{2,1,0:T(8,128)} %copy.77), calls=%async_computation.3 | async-start | bytes 4194304 | tf_op jit(solution)/shard_map/all_to_all | solution.py:234
  209.7 10.5 %copy-start.3 = (f32[8,64,1024]{2,1,0:T(8,128)S(1)}, f32[8,64,1024]{2,1,0:T(8,128)}, u32[]{:S(2)}) copy-start(f32[8,64,1024]{2,1,0:T(8,128)} %param.6) | copy-start | bytes 6291460
  210.5 9.6 %copy-start.2 = (f32[8,64,1024]{2,1,0:T(8,128)S(1)}, f32[8,64,1024]{2,1,0:T(8,128)}, u32[]{:S(2)}) copy-start(f32[8,64,1024]{2,1,0:T(8,128)} %param.8) | copy-start | bytes 6291460
  210.6 3.7 %collective-permute-start = (f32[1,64,1024]{2,1,0:T(8,128)S(1)}, f32[1,64,1024]{2,1,0:T(8,128)S(1)}, u32[]{:S(2)}, u32[]{:S(2)}) collective-permute-start(f32[1,64,1024]{2,1,0:T(8,128)S(1)} %copy.79), channel_id=1, source_target_pairs={{0,4},{4,8},{8,12},{12,16},{16,20},{20,24},{24,28},{1,5},{5,9},{9,... | collective-permute-start | bytes 786440 | tf_op jit(solution)/shard_map/ppermute | solution.py:36
  212.0 4.1 %collective-permute-start.1 = (f32[8,1,1024]{2,0,1:T(8,128)S(1)}, f32[8,1,1024]{2,0,1:T(8,128)S(1)}, u32[]{:S(2)}, u32[]{:S(2)}) collective-permute-start(f32[8,1,1024]{2,0,1:T(8,128)S(1)} %get-tuple-element.31), channel_id=1, source_target_pairs={{1,0},{2,1},{3,2},{0,3},{5,4},{6,5},{7,6},{4,7},{9,8},{10,9},{11,1... | collective-permute-start | bytes 98312 | tf_op jit(solution)/shard_map/ppermute | solution.py:28
  214.1 6.0 %collective-permute-start.2 = (f32[8,1,1024]{2,0,1:T(8,128)S(1)}, f32[8,1,1024]{2,0,1:T(8,128)S(1)}, u32[]{:S(2)}, u32[]{:S(2)}) collective-permute-start(f32[8,1,1024]{2,0,1:T(8,128)S(1)} %get-tuple-element.32), channel_id=1, source_target_pairs={{0,1},{1,2},{2,3},{3,0},{4,5},{5,6},{6,7},{7,4},{8,9},{9,10},{10,1... | collective-permute-start | bytes 98312 | tf_op jit(solution)/shard_map/ppermute | solution.py:25

commit v2 on v1

--- a/solution.py
+++ b/solution.py
@@ -235,6 +235,274 @@
     return restored / own_weights[:, None, None]
 
 
+LANES = 128
+
+
+def block_kernel(
+    z_count, t_count, shift_ref, signed_ref, spec_ref, base_ref, mob_ref, out_ref,
+    state, gain, cross, start_val, z_sent, z_halo, c_sent, c_halo,
+    z_send, z_recv, c_send, c_recv,
+):
+    coefs, rows, cols = spec_ref.shape
+    tiles = rows // TILE
+    per = LANES // tiles
+    groups = coefs // per
+    keep = 1.0 - damping
+    z_me, t_me = lax.axis_index("space"), lax.axis_index("tm")
+    z_to = (lax.rem(z_me + z_count - 1, z_count), lax.rem(z_me + 1, z_count))
+    t_to = (lax.rem(t_me + t_count - 1, t_count), lax.rem(t_me + 1, t_count))
+    lane = lax.broadcasted_iota(jnp.int32, (TILE, LANES), 1)
+    order = [0, tiles - 1] + list(range(1, tiles - 1))
+
+    barrier = pltpu.get_barrier_semaphore()
+    for axis, others in (("space", z_to), ("tm", t_to)):
+        for other in others:
+            pl.semaphore_signal(
+                barrier, inc=1, device_id={axis: other}, device_id_type=pl.DeviceIdType.MESH
+            )
+    pl.semaphore_wait(barrier, 4)
+
+    def copies(slot, g):
+        made = []
+        for axis, to, src, dst, snd, rcv in (
+            ("space", z_to, z_sent, z_halo, z_send, z_recv),
+            ("tm", t_to, c_sent, c_halo, c_send, c_recv),
+        ):
+            for side in range(2):
+                made.append(
+                    pltpu.make_async_remote_copy(
+                        src_ref=src.at[slot, g, side],
+                        dst_ref=dst.at[slot, g, 1 - side],
+                        send_sem=snd.at[slot, g, side],
+                        recv_sem=rcv.at[slot, g, 1 - side],
+                        device_id={axis: to[side]},
+                        device_id_type=pl.DeviceIdType.MESH,
+                    )
+                )
+        return made
+
+    def keep_edges(slot, g, i, t, value, low, high):
+        if t == 0:
+            z_sent[slot, g, 0, i : i + 1, :] = value[0:1]
+        if t == tiles - 1:
+            z_sent[slot, g, 1, i : i + 1, :] = value[TILE - 1 :]
+        k = t * per + i
+        turned = pltpu.roll(value, k, 1) if k else value
+        low = jnp.where(lane == k, turned, low)
+        high = jnp.where(lane == (k - 1) % LANES, turned, high)
+        return low, high
+
+    def prepare(g, _):
+        low = high = jnp.zeros((TILE, LANES), jnp.float32)
+        for p in range(per // 2):
+            q = g * (per // 2) + p
+            sig_e, sig_o = shift_ref[2 * q], shift_ref[2 * q + 1]
+            c_e = signed_ref[2 * q]
+            for t in order:
+                span = pl.ds(t * TILE, TILE)
+                mob, base = mob_ref[span, :], base_ref[span, :]
+                d_e, d_o = sig_e + base, sig_o + base
+                scale = damping / (d_e * d_o + c_e * c_e)
+                s_e, s_o = spec_ref[2 * q, span, :], spec_ref[2 * q + 1, span, :]
+                b_e = scale * (d_o * s_e - c_e * s_o)
+                b_o = scale * (d_e * s_o + c_e * s_e)
+                scaled = scale * mob
+                gain[2 * q, span, :] = scaled * d_o
+                gain[2 * q + 1, span, :] = scaled * d_e
+                cross[q, span, :] = scaled * c_e
+                start_val[2 * q, span, :] = b_e
+                start_val[2 * q + 1, span, :] = b_o
+                own = pl.ds((t + 1) * TILE, TILE)
+                state[0, 2 * q, own, :] = b_e
+                state[0, 2 * q + 1, own, :] = b_o
+                low, high = keep_edges(0, g, 2 * p, t, b_e, low, high)
+                low, high = keep_edges(0, g, 2 * p + 1, t, b_o, low, high)
+        c_sent[0, g, 0] = low
+        c_sent[0, g, 1] = high
+        for copy in copies(0, g):
+            copy.start()
+        return 0
+
+    lax.fori_loop(0, groups, prepare, 0)
+
+    def sweep(s, _):
+        now = lax.rem(s, 2)
+        later = 1 - now
+
+        def one_group(g, _):
+            for copy in copies(now, g):
+                copy.wait()
+            from_left, from_right = c_halo[now, g, 0], c_halo[now, g, 1]
+            low = high = jnp.zeros((TILE, LANES), jnp.float32)
+
+            def around(m, i, t):
+                top = (t + 1) * TILE
+                mid = state[now, m, pl.ds(top, TILE), :]
+                k = t * per + i
+                edge = jnp.where(lane == k, from_right, from_left)
+                edge = pltpu.roll(edge, LANES - k, 1) if k else edge
+                total = state[now, m, pl.ds(top - 1, TILE), :] + state[now, m, pl.ds(top + 1, TILE), :]
+                right = pltpu.roll(jnp.where(lane == 0, edge, mid), LANES - 1, 1)
+                left = pltpu.roll(jnp.where(lane == LANES - 1, edge, mid), 1, 1)
+                return mid, total + (left + right)
+
+            for p in range(per // 2):
+                q = g * (per // 2) + p
+                for part in range(2):
+                    i = 2 * p + part
+                    state[now, 2 * q + part, pl.ds(TILE - 1, 1), :] = z_halo[now, g, 0, i : i + 1, :]
+                    state[now, 2 * q + part, pl.ds(TILE + rows, 1), :] = z_halo[now, g, 1, i : i + 1, :]
+                for t in order:
+                    span = pl.ds(t * TILE, TILE)
+                    own = pl.ds((t + 1) * TILE, TILE)
+                    y_e, n_e = around(2 * q, 2 * p, t)
+                    y_o, n_o = around(2 * q + 1, 2 * p + 1, t)
+                    c = cross[q, span, :]
+                    new_e = keep * y_e + start_val[2 * q, span, :] + (gain[2 * q, span, :] * n_e - c * n_o)
+                    new_o = keep * y_o + start_val[2 * q + 1, span, :] + (gain[2 * q + 1, span, :] * n_o + c * n_e)
+                    state[later, 2 * q, own, :] = new_e
+                    state[later, 2 * q + 1, own, :] = new_o
+                    low, high = keep_edges(later, g, 2 * p, t, new_e, low, high)
+                    low, high = keep_edges(later, g, 2 * p + 1, t, new_o, low, high)
+            c_sent[later, g, 0] = low
+            c_sent[later, g, 1] = high
+
+            @pl.when(s < SWEEPS - 2)
+            def _():
+                for copy in copies(later, g):
+                    copy.start()
+
+            return 0
+
+        return lax.fori_loop(0, groups, one_group, 0)
+
+    lax.fori_loop(0, SWEEPS - 1, sweep, 0)
+    last = (SWEEPS - 1) % 2
+
+    def store(m, _):
+        out_ref[m] = state[last, m, TILE : TILE + rows, :]
+        return 0
+
+    lax.fori_loop(0, coefs, store, 0)
+
+
+def fits_block(coefs, rows, cols):
+    tiles = rows // TILE
+    return (
+        cols == LANES and rows % TILE == 0 and LANES % tiles == 0
+        and (LANES // tiles) % 8 == 0 and coefs % (LANES // tiles) == 0
+    )
+
+
+def relax_block(spectrum, shifts, signed, frozen, mobility):
+    coefs, rows, cols = spectrum.shape
+    per = LANES // (rows // TILE)
+    groups = coefs // per
+    vmem = pl.BlockSpec(memory_space=pltpu.VMEM)
+    smem = pl.BlockSpec(memory_space=pltpu.SMEM)
+    sems = pltpu.SemaphoreType.DMA((2, groups, 2))
+    return pl.pallas_call(
+        functools.partial(block_kernel, lax.axis_size("space"), lax.axis_size("tm")),
+        out_shape=jax.ShapeDtypeStruct(spectrum.shape, jnp.float32),
+        in_specs=[smem, smem, vmem, vmem, vmem],
+        out_specs=vmem,
+        scratch_shapes=[
+            pltpu.VMEM((2, coefs, rows + 2 * TILE, cols), jnp.float32),
+            pltpu.VMEM((coefs, rows, cols), jnp.float32),
+            pltpu.VMEM((coefs // 2, rows, cols), jnp.float32),
+            pltpu.VMEM((coefs, rows, cols), jnp.float32),
+            pltpu.VMEM((2, groups, 2, per, cols), jnp.float32),
+            pltpu.VMEM((2, groups, 2, per, cols), jnp.float32),
+            pltpu.VMEM((2, groups, 2, TILE, LANES), jnp.float32),
+            pltpu.VMEM((2, groups, 2, TILE, LANES), jnp.float32),
+            sems, sems, sems, sems,
+        ],
+        compiler_params=pltpu.CompilerParams(
+            collective_id=1, has_side_effects=True, vmem_limit_bytes=32 * 1024 * 1024
+        ),
+    )(shifts, signed, spectrum, frozen + 4.0 * mobility, mobility)
+
+
+def precondition_columns(values, frozen, mobility, tables):
+    forward, inverse, shifts, signed, weights = tables
+    width = values.shape[2] // lax.axis_size("tm")
+    first = lax.axis_index("tm") * width
+    own_frozen = lax.dynamic_slice_in_dim(frozen, first, width, axis=1)
+    own_mobility = lax.dynamic_slice_in_dim(mobility, first, width, axis=1)
+    weighted = forward * weights[None, :]
+    gathered = lax.all_to_all(values, "tm", split_axis=2, concat_axis=0, tiled=True)
+    spectrum = jnp.einsum("mj,jrc->mrc", weighted, gathered, precision=lax.Precision.HIGHEST)
+    solved = relax_block(spectrum, shifts, signed, own_frozen, own_mobility)
+    restoring = inverse / weights[:, None]
+    in_time = jnp.einsum("jm,mrc->jrc", restoring, solved, precision=lax.Precision.HIGHEST)
+    return lax.all_to_all(in_time, "tm", split_axis=0, concat_axis=2, tiled=True)
+
+
+def sum_kernel(t_count, z_count, x_ref, out_ref, t_got, z_own, z_got, t_send, t_recv, z_send, z_recv):
+    barrier = pltpu.get_barrier_semaphore()
+    places = (("tm", t_count), ("space", z_count))
+    for axis, count in places:
+        me = lax.axis_index(axis)
+        for k in range(1, count):
+            pl.semaphore_signal(
+                barrier, inc=1, device_id={axis: lax.rem(me + k, count)},
+                device_id_type=pl.DeviceIdType.MESH,
+            )
+    pl.semaphore_wait(barrier, t_count + z_count - 2)
+    for axis, count, src, got, snd, rcv in (
+        ("tm", t_count, x_ref, t_got, t_send, t_recv),
+        ("space", z_count, z_own, z_got, z_send, z_recv),
+    ):
+        me = lax.axis_index(axis)
+        made = []
+        for k in range(1, count):
+            made.append(
+                pltpu.make_async_remote_copy(
+                    src_ref=src, dst_ref=got.at[me], send_sem=snd.at[k], recv_sem=rcv.at[k],
+                    device_id={axis: lax.rem(me + k, count)},
+                    device_id_type=pl.DeviceIdType.MESH,
+                )
+            )
+        for copy in made:
+            copy.start()
+        got[me] = src[...]
+        for copy in made:
+            copy.wait()
+        total = got[0]
+        for k in range(1, count):
+            total = total + got[k]
+        if axis == "tm":
+            z_own[...] = total
+        else:
+            out_ref[...] = total
+
+
+def summed(parts):
+    t_count, z_count = lax.axis_size("tm"), lax.axis_size("space")
+    row = lax.broadcasted_iota(jnp.int32, (TILE, LANES), 0)
+    packed = jnp.zeros((TILE, LANES), jnp.float32)
+    for k, part in enumerate(parts):
+        packed = jnp.where(row == k, part, packed)
+    vmem = pl.BlockSpec(memory_space=pltpu.VMEM)
+    dma = pltpu.SemaphoreType.DMA
+    total = pl.pallas_call(
+        functools.partial(sum_kernel, t_count, z_count),
+        out_shape=jax.ShapeDtypeStruct((TILE, LANES), jnp.float32),
+        in_specs=[vmem],
+        out_specs=vmem,
+        scratch_shapes=[
+            pltpu.VMEM((t_count, TILE, LANES), jnp.float32),
+            pltpu.VMEM((TILE, LANES), jnp.float32),
+            pltpu.VMEM((z_count, TILE, LANES), jnp.float32),
+            dma((t_count,)), dma((t_count,)), dma((z_count,)), dma((z_count,)),
+        ],
+        compiler_params=pltpu.CompilerParams(
+            collective_id=2, has_side_effects=True, vmem_limit_bytes=4 * 1024 * 1024
+        ),
+    )(packed)
+    return [total[k, 0] for k in range(len(parts))]
+
+
 def jacobian(values, trajectory, mobility):
     arriving = passed_along(values[-1:], "tm", 1)
     earlier = jnp.concatenate([arriving, values[:-1]], axis=0)
@@ -245,11 +513,14 @@
 def on_device(trajectory, initial_state, residual, mobility):
     tables = time_tables(NT)
     frozen = reaction_scale * jnp.maximum(3.0 * initial_state * initial_state - 1.0, 0.0)
-    direction = precondition(residual, frozen, mobility, tables)
+    steps_dev, rows, cols = residual.shape
+    shards = lax.axis_size("tm")
+    by_columns = cols % shards == 0 and fits_block(NT, rows, cols // shards)
+    run = precondition_columns if by_columns else precondition
+    direction = run(residual, frozen, mobility, tables)
     applied = jacobian(direction, trajectory, mobility)
-    norm_square, cross_sum, squared_applied = lax.psum(
-        (jnp.sum(residual * residual), jnp.sum(residual * applied), jnp.sum(applied * applied)),
-        ("tm", "space"),
+    norm_square, cross_sum, squared_applied = summed(
+        (jnp.sum(residual * residual), jnp.sum(residual * applied), jnp.sum(applied * applied))
     )
     projection = cross_sum / norm_square
     squared_sum = squared_applied / norm_square

time: 274 us -> 448 us (1.64)
  Pallas kernels: 66.2 us -> 322 us
  waiting for transfers between devices: 109 us -> 57.3 us
  blocking collectives: 37.1 us -> 0 us
  local copies, waits for them, and re-layouts: 15.5 us -> 25.8 us
  starting transfers between devices: 20.7 us -> 13.5 us
    pallas_call x1 -> x2, Pallas kernels: 66.2 us -> 322 us  [the longest x1 314 us: relax_block(): pl.pallas_call(functools.partial(block_kernel, lax.axis_size('space'), la...]
    all_to_all x4 -> x2, waiting for transfers between devices: 104 us -> 51.4 us  [the longest x1 26.5 us: precondition_columns(): lax.all_to_all(in_time, 'tm', split_axis=0, concat_axis=2, tiled=True)]
    psum x1 -> x0, blocking collectives: 37.1 us -> none  [on_device(): lax.psum((jnp.sum(residual * residual), jnp.sum(residual * applied), jnp....]
    unnamed x11, local copies, waits for them, and re-layouts: 2.56 us -> 16 us
    all_to_all x4 -> x2, starting transfers between devices: 17.2 us -> 8.94 us  [the longest x1 5.33 us: precondition_columns(): lax.all_to_all(values, 'tm', split_axis=2, concat_axis=0, tiled=True)]
    all_to_all x0 -> x1, other arithmetic: none -> 7.22 us  [precondition_columns(): lax.all_to_all(values, 'tm', split_axis=2, concat_axis=0, tiled=True)]
  transfers between devices with their start and end apart: 7 -> 5, of which waited for: 6 -> 4; matrix products, arithmetic and copies ran while one was open for 1% -> 1% of each run, Pallas kernels for 0% -> 0%
where the time goes in v2:
time: 448 us; the launch traced here: 447 us
  Pallas kernels  322 us (72%)
  waiting for transfers between devices  57.3 us (13%)
  local copies, waits for them, and re-layouts  25.8 us (6%)
  other arithmetic  15 us (3%)
  starting transfers between devices  13.5 us (3%)
  between operations  7.34 us (2%)
  matrix products  6.15 us (1%)
    pallas_call x1, Pallas kernels, relax_block(): pl.pallas_call(functools.partial(block_kernel, lax.axis_size('space'), la...  314 us
    all_to_all x1, waiting for transfers between devices, precondition_columns(): lax.all_to_all(in_time, 'tm', split_axis=0, concat_axis=2, tiled=True)  26.5 us
    all_to_all x1, waiting for transfers between devices, precondition_columns(): lax.all_to_all(values, 'tm', split_axis=2, concat_axis=0, tiled=True)  24.9 us
    unnamed x11, local copies, waits for them, and re-layouts  16 us
  transfers between devices with their start and end apart: 5, of which 4 were waited for; matrix products, arithmetic and copies ran while one was open for 1% of the time, Pallas kernels for 0%

profile of v2, /device:TPU:0, one launch (start us, length us, event | category | flops | bytes accessed | tf_op | source)
XLA Modules:
  0.0 447.1 jit_solution(17428270465804082118)
XLA Ops:
  0.6 3.8 copy.37
  4.5 7.2 %reshape.257 = f32[8,1,65536]{2,1,0:T(1,128)} reshape(f32[1024,8,64]{2,1,0:T(8,128)} %bitcast.46) | data formatting | bytes 4194304
  11.7 5.3 %all-to-all-start = ((f32[8,1,65536]{2,1,0:T(1,128)}), f32[8,1,65536]{2,1,0:T(1,128)S(1)}, u32[]{:S(2)}, u32[]{:S(2)}) async-start(f32[8,1,65536]{2,1,0:T(1,128)} %reshape.257), calls=%async_computation | async-start | bytes 4194304 | tf_op jit(solution)/shard_map/all_to_all | solution.py:433
  17.6 0.1 multiply_cosine_fusion
  18.0 0.8 constant_dynamic-slice_fusion
  18.7 24.9 %all-to-all-done = f32[8,1,65536]{2,1,0:T(1,128)S(1)} async-done(((f32[8,1,65536]{2,1,0:T(1,128)}), f32[8,1,65536]{2,1,0:T(1,128)S(1)}, u32[]{:S(2)}, u32[]{:S(2)}) %all-to-all-start) | async-done | bytes 2097184 | tf_op jit(solution)/shard_map/all_to_all | solution.py:433
  43.6 1.3 copy-done.1
  44.9 0.5 broadcast.268
  45.4 7.2 %reduce.2 = f32[8,65536]{1,0:T(8,128)S(1)} reduce(f32[8,1,65536]{2,1,0:T(1,128)} %copy-done.1, f32[]{:T(128)} %broadcast.268), dimensions={1}, to_apply=%all_to_all.26.reduce_sub_computation | reduce | bytes 4194308 | tf_op jit(solution)/shard_map/all_to_all | solution.py:433
  52.7 3.6 reshape.258
  56.3 3.0 copy.39
  59.3 3.0 fusion.13
  62.3 1.2 copy.41.spec_ref
  63.6 313.7 %shard_map.59 = f32[64,64,128]{2,1,0:T(8,128)S(1)} custom-call(f32[64]{0:T(128)S(1)} %constant_dynamic-update-slice_fusion.shift_ref, f32[64]{0:T(128)S(1)} %reshape.254.signed_ref, f32[64,64,128]{2,1,0:T(8,128)S(1)} %copy.41.spec_ref, f32[64,128]{1,0:T(8,128)S(1)} %get-tuple-element.24.base_ref, f32[64,128]{1,0:T(8,128)S(1)} %get-tuple-element.23.mob_ref), custom_call_target="tpu_custom_call" | custom-call | tf_op jit(solution)/shard_map/pallas_call | solution.py:404
  377.3 3.1 fusion.11
  380.4 2.5 copy.44
  382.9 3.6 all-to-all-start.1
  386.5 26.5 %all-to-all-done.1 = f32[64,64,128]{2,1,0:T(8,128)S(1)} async-done(((f32[64,64,128]{2,1,0:T(8,128)}), f32[64,64,128]{2,1,0:T(8,128)S(1)}, u32[]{:S(2)}, u32[]{:S(2)}) %all-to-all-start.1) | async-done | bytes 2097184 | tf_op jit(solution)/shard_map/all_to_all | solution.py:438
  413.1 0.2 copy_bitcast_fusion.1
  413.3 1.3 collective-permute-start
  414.7 0.3 copy.64
  415.0 0.8 fusion.30
  415.9 3.2 collective-permute-start.1
  419.1 0.1 fusion.31
  419.2 1.4 collective-permute-done.1
  420.7 4.4 collective-permute-done.2
  425.1 3.0 multiply_reduce_fusion.2
  428.2 0.6 compare_select_fusion
  428.8 1.4 select_select_fusion.x_ref
  430.2 8.3 %shard_map.60 = f32[8,128]{1,0:T(8,128)S(1)} custom-call(f32[8,128]{1,0:T(8,128)S(1)} %select_select_fusion.x_ref), custom_call_target="tpu_custom_call" | custom-call | tf_op jit(solution)/shard_map/pallas_call | solution.py:488
  438.4 0.5 fusion.33
  444.3 1.6 broadcast_multiply_fusion
  (30 shorter events, 0.8 us)
Async XLA Ops:
  11.7 6.3 %copy-start.3 = (f32[64,1024]{1,0:T(8,128)S(1)}, f32[64,1024]{1,0:T(8,128)}, u32[]{:S(2)}) copy-start(f32[64,1024]{1,0:T(8,128)} %param.9) | copy-start | bytes 786436
  11.7 31.9 %all-to-all-start = ((f32[8,1,65536]{2,1,0:T(1,128)}), f32[8,1,65536]{2,1,0:T(1,128)S(1)}, u32[]{:S(2)}, u32[]{:S(2)}) async-start(f32[8,1,65536]{2,1,0:T(1,128)} %reshape.257), calls=%async_computation | async-start | bytes 4194304 | tf_op jit(solution)/shard_map/all_to_all | solution.py:433
  43.6 1.3 copy-start.1
  382.9 30.2 %all-to-all-start.1 = ((f32[64,64,128]{2,1,0:T(8,128)}), f32[64,64,128]{2,1,0:T(8,128)S(1)}, u32[]{:S(2)}, u32[]{:S(2)}) async-start(f32[64,64,128]{2,1,0:T(8,128)} %copy.44), calls=%async_computation.1 | async-start | bytes 4194304 | tf_op jit(solution)/shard_map/all_to_all | solution.py:438
  413.3 11.8 %collective-permute-start = (f32[1,64,1024]{2,1,0:T(8,128)S(1)}, f32[1,64,1024]{2,1,0:T(8,128)S(1)}, u32[]{:S(2)}, u32[]{:S(2)}) collective-permute-start(f32[1,64,1024]{2,1,0:T(8,128)S(1)} %copy_bitcast_fusion.2), channel_id=1, source_target_pairs={{0,4},{4,8},{8,12},{12,16},{16,20},{20,24},{24,28},{1,5},{5,9},{9,... | collective-permute-start | bytes 786440 | tf_op jit(solution)/shard_map/ppermute | solution.py:36
  414.9 10.2 %copy-start = (f32[8,64,1024]{2,1,0:T(8,128)S(1)}, f32[8,64,1024]{2,1,0:T(8,128)}, u32[]{:S(2)}) copy-start(f32[8,64,1024]{2,1,0:T(8,128)} %param.8) | copy-start | bytes 6291460
  414.9 10.2 %copy-start.2 = (f32[8,64,1024]{2,1,0:T(8,128)S(1)}, f32[8,64,1024]{2,1,0:T(8,128)}, u32[]{:S(2)}) copy-start(f32[8,64,1024]{2,1,0:T(8,128)} %param.6) | copy-start | bytes 6291460
  415.9 4.8 %collective-permute-start.1 = (f32[8,1,1024]{2,1,0:T(1,128)S(1)}, f32[8,1,1024]{2,1,0:T(1,128)S(1)}, u32[]{:S(2)}, u32[]{:S(2)}) collective-permute-start(f32[8,1,1024]{2,1,0:T(1,128)S(1)} %get-tuple-element.21), channel_id=1, source_target_pairs={{1,0},{2,1},{3,2},{0,3},{5,4},{6,5},{7,6},{4,7},{9,8},{10,9},{11,1... | collective-permute-start | bytes 98312 | tf_op jit(solution)/shard_map/ppermute | solution.py:28
  419.1 6.0 %collective-permute-start.2 = (f32[8,1,1024]{2,1,0:T(1,128)S(1)}, f32[8,1,1024]{2,1,0:T(1,128)S(1)}, u32[]{:S(2)}, u32[]{:S(2)}) collective-permute-start(f32[8,1,1024]{2,1,0:T(1,128)S(1)} %get-tuple-element.22), channel_id=1, source_target_pairs={{0,1},{1,2},{2,3},{3,0},{4,5},{5,6},{6,7},{7,4},{8,9},{9,10},{10,1... | collective-permute-start | bytes 98312 | tf_op jit(solution)/shard_map/ppermute | solution.py:25

commit v3 on v2

--- a/solution.py
+++ b/solution.py
@@ -240,7 +240,7 @@
 
 def block_kernel(
     z_count, t_count, shift_ref, signed_ref, spec_ref, base_ref, mob_ref, out_ref,
-    state, gain, cross, start_val, z_sent, z_halo, c_sent, c_halo,
+    state_a, state_b, gain, cross, start_val, z_sent, z_halo, c_sent, c_halo,
     z_send, z_recv, c_send, c_recv,
 ):
     coefs, rows, cols = spec_ref.shape
@@ -313,8 +313,8 @@
                 start_val[2 * q, span, :] = b_e
                 start_val[2 * q + 1, span, :] = b_o
                 own = pl.ds((t + 1) * TILE, TILE)
-                state[0, 2 * q, own, :] = b_e
-                state[0, 2 * q + 1, own, :] = b_o
+                state_a[2 * q, own, :] = b_e
+                state_a[2 * q + 1, own, :] = b_o
                 low, high = keep_edges(0, g, 2 * p, t, b_e, low, high)
                 low, high = keep_edges(0, g, 2 * p + 1, t, b_o, low, high)
         c_sent[0, g, 0] = low
@@ -325,8 +325,7 @@
 
     lax.fori_loop(0, groups, prepare, 0)
 
-    def sweep(s, _):
-        now = lax.rem(s, 2)
+    def sweep(now, source, target, send):
         later = 1 - now
 
         def one_group(g, _):
@@ -334,53 +333,65 @@
                 copy.wait()
             from_left, from_right = c_halo[now, g, 0], c_halo[now, g, 1]
             low = high = jnp.zeros((TILE, LANES), jnp.float32)
+            for i in range(per):
+                m = g * per + i
+                source[m, pl.ds(TILE - 1, 1), :] = z_halo[now, g, 0, i : i + 1, :]
+                source[m, pl.ds(TILE + rows, 1), :] = z_halo[now, g, 1, i : i + 1, :]
 
             def around(m, i, t):
                 top = (t + 1) * TILE
-                mid = state[now, m, pl.ds(top, TILE), :]
+                mid = source[m, pl.ds(top, TILE), :]
                 k = t * per + i
                 edge = jnp.where(lane == k, from_right, from_left)
                 edge = pltpu.roll(edge, LANES - k, 1) if k else edge
-                total = state[now, m, pl.ds(top - 1, TILE), :] + state[now, m, pl.ds(top + 1, TILE), :]
+                total = source[m, pl.ds(top - 1, TILE), :] + source[m, pl.ds(top + 1, TILE), :]
                 right = pltpu.roll(jnp.where(lane == 0, edge, mid), LANES - 1, 1)
                 left = pltpu.roll(jnp.where(lane == LANES - 1, edge, mid), 1, 1)
                 return mid, total + (left + right)
 
             for p in range(per // 2):
                 q = g * (per // 2) + p
-                for part in range(2):
-                    i = 2 * p + part
-                    state[now, 2 * q + part, pl.ds(TILE - 1, 1), :] = z_halo[now, g, 0, i : i + 1, :]
-                    state[now, 2 * q + part, pl.ds(TILE + rows, 1), :] = z_halo[now, g, 1, i : i + 1, :]
-                for t in order:
+                news = []
+                for t in range(tiles):
                     span = pl.ds(t * TILE, TILE)
-                    own = pl.ds((t + 1) * TILE, TILE)
                     y_e, n_e = around(2 * q, 2 * p, t)
                     y_o, n_o = around(2 * q + 1, 2 * p + 1, t)
                     c = cross[q, span, :]
                     new_e = keep * y_e + start_val[2 * q, span, :] + (gain[2 * q, span, :] * n_e - c * n_o)
                     new_o = keep * y_o + start_val[2 * q + 1, span, :] + (gain[2 * q + 1, span, :] * n_o + c * n_e)
-                    state[later, 2 * q, own, :] = new_e
-                    state[later, 2 * q + 1, own, :] = new_o
-                    low, high = keep_edges(later, g, 2 * p, t, new_e, low, high)
-                    low, high = keep_edges(later, g, 2 * p + 1, t, new_o, low, high)
-            c_sent[later, g, 0] = low
-            c_sent[later, g, 1] = high
-
-            @pl.when(s < SWEEPS - 2)
-            def _():
+                    news.append((new_e, new_o))
+                for t, (new_e, new_o) in enumerate(news):
+                    own = pl.ds((t + 1) * TILE, TILE)
+                    target[2 * q, own, :] = new_e
+                    target[2 * q + 1, own, :] = new_o
+                    if send:
+                        low, high = keep_edges(later, g, 2 * p, t, new_e, low, high)
+                        low, high = keep_edges(later, g, 2 * p + 1, t, new_o, low, high)
+            if send:
+                c_sent[later, g, 0] = low
+                c_sent[later, g, 1] = high
                 for copy in copies(later, g):
                     copy.start()
-
             return 0
 
-        return lax.fori_loop(0, groups, one_group, 0)
-
-    lax.fori_loop(0, SWEEPS - 1, sweep, 0)
-    last = (SWEEPS - 1) % 2
+        lax.fori_loop(0, groups, one_group, 0)
+
+    def two_sweeps(s, _):
+        sweep(0, state_a, state_b, True)
+        sweep(1, state_b, state_a, True)
+        return 0
+
+    count = SWEEPS - 1
+    lax.fori_loop(0, (count - 1) // 2, two_sweeps, 0)
+    if count % 2 == 0:
+        sweep(0, state_a, state_b, True)
+        sweep(1, state_b, state_a, False)
+    else:
+        sweep(0, state_a, state_b, False)
+    last = state_b if count % 2 else state_a
 
     def store(m, _):
-        out_ref[m] = state[last, m, TILE : TILE + rows, :]
+        out_ref[m] = last[m, TILE : TILE + rows, :]
         return 0
 
     lax.fori_loop(0, coefs, store, 0)
@@ -407,7 +418,8 @@
         in_specs=[smem, smem, vmem, vmem, vmem],
         out_specs=vmem,
         scratch_shapes=[
-            pltpu.VMEM((2, coefs, rows + 2 * TILE, cols), jnp.float32),
+            pltpu.VMEM((coefs, rows + 2 * TILE, cols), jnp.float32),
+            pltpu.VMEM((coefs, rows + 2 * TILE, cols), jnp.float32),
             pltpu.VMEM((coefs, rows, cols), jnp.float32),
             pltpu.VMEM((coefs // 2, rows, cols), jnp.float32),
             pltpu.VMEM((coefs, rows, cols), jnp.float32),

time: 448 us -> 486 us (1.085)
  Pallas kernels: 322 us -> 360 us
    pallas_call x1, Pallas kernels: 314 us -> 351 us  [relax_block(): pl.pallas_call(functools.partial(block_kernel, lax.axis_size('space'), la...]
where the time goes in v3:
time: 486 us; the launch traced here: 485 us
  Pallas kernels  360 us (74%)
  waiting for transfers between devices  57.3 us (12%)
  local copies, waits for them, and re-layouts  25.8 us (5%)
  other arithmetic  15 us (3%)
  starting transfers between devices  13.7 us (3%)
  between operations  7.34 us (2%)
  matrix products  6.15 us (1%)
    pallas_call x1, Pallas kernels, relax_block(): pl.pallas_call(functools.partial(block_kernel, lax.axis_size('space'), la...  351 us
    all_to_all x1, waiting for transfers between devices, precondition_columns(): lax.all_to_all(in_time, 'tm', split_axis=0, concat_axis=2, tiled=True)  26.5 us
    all_to_all x1, waiting for transfers between devices, precondition_columns(): lax.all_to_all(values, 'tm', split_axis=2, concat_axis=0, tiled=True)  24.9 us
    unnamed x11, local copies, waits for them, and re-layouts  16 us
  transfers between devices with their start and end apart: 5, of which 4 were waited for; matrix products, arithmetic and copies ran while one was open for 1% of the time, Pallas kernels for 0%

profile of v3, /device:TPU:0, one launch (start us, length us, event | category | flops | bytes accessed | tf_op | source)
XLA Modules:
  0.0 484.9 jit_solution(911524260893556137)
XLA Ops:
  0.6 3.8 copy.37
  4.5 7.2 %reshape.257 = f32[8,1,65536]{2,1,0:T(1,128)} reshape(f32[1024,8,64]{2,1,0:T(8,128)} %bitcast.46) | data formatting | bytes 4194304
  11.7 5.3 %all-to-all-start = ((f32[8,1,65536]{2,1,0:T(1,128)}), f32[8,1,65536]{2,1,0:T(1,128)S(1)}, u32[]{:S(2)}, u32[]{:S(2)}) async-start(f32[8,1,65536]{2,1,0:T(1,128)} %reshape.257), calls=%async_computation | async-start | bytes 4194304 | tf_op jit(solution)/shard_map/all_to_all | solution.py:445
  17.6 0.1 multiply_cosine_fusion
  18.0 0.8 constant_dynamic-slice_fusion
  18.7 24.9 %all-to-all-done = f32[8,1,65536]{2,1,0:T(1,128)S(1)} async-done(((f32[8,1,65536]{2,1,0:T(1,128)}), f32[8,1,65536]{2,1,0:T(1,128)S(1)}, u32[]{:S(2)}, u32[]{:S(2)}) %all-to-all-start) | async-done | bytes 2097184 | tf_op jit(solution)/shard_map/all_to_all | solution.py:445
  43.6 1.3 copy-done.1
  44.9 0.5 broadcast.268
  45.4 7.2 %reduce.2 = f32[8,65536]{1,0:T(8,128)S(1)} reduce(f32[8,1,65536]{2,1,0:T(1,128)} %copy-done.1, f32[]{:T(128)} %broadcast.268), dimensions={1}, to_apply=%all_to_all.26.reduce_sub_computation | reduce | bytes 4194308 | tf_op jit(solution)/shard_map/all_to_all | solution.py:445
  52.7 3.6 reshape.258
  56.3 3.0 copy.39
  59.3 3.0 fusion.13
  62.3 1.2 copy.41.spec_ref
  63.6 351.3 %shard_map.59 = f32[64,64,128]{2,1,0:T(8,128)S(1)} custom-call(f32[64]{0:T(128)S(1)} %constant_dynamic-update-slice_fusion.shift_ref, f32[64]{0:T(128)S(1)} %reshape.254.signed_ref, f32[64,64,128]{2,1,0:T(8,128)S(1)} %copy.41.spec_ref, f32[64,128]{1,0:T(8,128)S(1)} %get-tuple-element.24.base_ref, f32[64,128]{1,0:T(8,128)S(1)} %get-tuple-element.23.mob_ref), custom_call_target="tpu_custom_call" | custom-call | tf_op jit(solution)/shard_map/pallas_call | solution.py:415
  414.9 3.1 fusion.11
  418.0 2.5 copy.44
  420.5 3.6 all-to-all-start.1
  424.2 26.5 %all-to-all-done.1 = f32[64,64,128]{2,1,0:T(8,128)S(1)} async-done(((f32[64,64,128]{2,1,0:T(8,128)}), f32[64,64,128]{2,1,0:T(8,128)S(1)}, u32[]{:S(2)}, u32[]{:S(2)}) %all-to-all-start.1) | async-done | bytes 2097184 | tf_op jit(solution)/shard_map/all_to_all | solution.py:450
  450.7 0.2 copy_bitcast_fusion.1
  451.0 1.5 collective-permute-start
  452.5 0.3 copy.64
  452.8 0.8 fusion.30
  453.7 3.2 collective-permute-start.1
  456.9 0.1 fusion.31
  457.1 1.4 collective-permute-done.1
  458.5 4.4 collective-permute-done.2
  463.0 3.0 multiply_reduce_fusion.2
  466.0 0.6 compare_select_fusion
  466.6 1.4 select_select_fusion.x_ref
  468.0 8.3 %shard_map.60 = f32[8,128]{1,0:T(8,128)S(1)} custom-call(f32[8,128]{1,0:T(8,128)S(1)} %select_select_fusion.x_ref), custom_call_target="tpu_custom_call" | custom-call | tf_op jit(solution)/shard_map/pallas_call | solution.py:500
  476.3 0.5 fusion.33
  482.2 1.6 broadcast_multiply_fusion
  (30 shorter events, 0.8 us)
Async XLA Ops:
  11.7 6.3 %copy-start.3 = (f32[64,1024]{1,0:T(8,128)S(1)}, f32[64,1024]{1,0:T(8,128)}, u32[]{:S(2)}) copy-start(f32[64,1024]{1,0:T(8,128)} %param.9) | copy-start | bytes 786436
  11.7 31.9 %all-to-all-start = ((f32[8,1,65536]{2,1,0:T(1,128)}), f32[8,1,65536]{2,1,0:T(1,128)S(1)}, u32[]{:S(2)}, u32[]{:S(2)}) async-start(f32[8,1,65536]{2,1,0:T(1,128)} %reshape.257), calls=%async_computation | async-start | bytes 4194304 | tf_op jit(solution)/shard_map/all_to_all | solution.py:445
  43.6 1.3 copy-start.1
  420.5 30.2 %all-to-all-start.1 = ((f32[64,64,128]{2,1,0:T(8,128)}), f32[64,64,128]{2,1,0:T(8,128)S(1)}, u32[]{:S(2)}, u32[]{:S(2)}) async-start(f32[64,64,128]{2,1,0:T(8,128)} %copy.44), calls=%async_computation.1 | async-start | bytes 4194304 | tf_op jit(solution)/shard_map/all_to_all | solution.py:450
  451.0 12.0 %collective-permute-start = (f32[1,64,1024]{2,1,0:T(8,128)S(1)}, f32[1,64,1024]{2,1,0:T(8,128)S(1)}, u32[]{:S(2)}, u32[]{:S(2)}) collective-permute-start(f32[1,64,1024]{2,1,0:T(8,128)S(1)} %copy_bitcast_fusion.2), channel_id=1, source_target_pairs={{0,4},{4,8},{8,12},{12,16},{16,20},{20,24},{24,28},{1,5},{5,9},{9,... | collective-permute-start | bytes 786440 | tf_op jit(solution)/shard_map/ppermute | solution.py:36
  452.8 10.2 %copy-start = (f32[8,64,1024]{2,1,0:T(8,128)S(1)}, f32[8,64,1024]{2,1,0:T(8,128)}, u32[]{:S(2)}) copy-start(f32[8,64,1024]{2,1,0:T(8,128)} %param.8) | copy-start | bytes 6291460
  452.8 10.2 %copy-start.2 = (f32[8,64,1024]{2,1,0:T(8,128)S(1)}, f32[8,64,1024]{2,1,0:T(8,128)}, u32[]{:S(2)}) copy-start(f32[8,64,1024]{2,1,0:T(8,128)} %param.6) | copy-start | bytes 6291460
  453.7 4.8 collective-permute-start.1
  456.9 6.0 %collective-permute-start.2 = (f32[8,1,1024]{2,1,0:T(1,128)S(1)}, f32[8,1,1024]{2,1,0:T(1,128)S(1)}, u32[]{:S(2)}, u32[]{:S(2)}) collective-permute-start(f32[8,1,1024]{2,1,0:T(1,128)S(1)} %get-tuple-element.22), channel_id=1, source_target_pairs={{0,1},{1,2},{2,3},{3,0},{4,5},{5,6},{6,7},{7,4},{8,9},{9,10},{10,1... | collective-permute-start | bytes 98312 | tf_op jit(solution)/shard_map/ppermute | solution.py:25

commit v4 on v1

--- a/solution.py
+++ b/solution.py
@@ -235,6 +235,74 @@
     return restored / own_weights[:, None, None]
 
 
+LANES = 128
+
+
+def sum_kernel(t_count, z_count, x_ref, out_ref, t_got, z_own, z_got, t_send, t_recv, z_send, z_recv):
+    barrier = pltpu.get_barrier_semaphore()
+    places = (("tm", t_count), ("space", z_count))
+    for axis, count in places:
+        me = lax.axis_index(axis)
+        for k in range(1, count):
+            pl.semaphore_signal(
+                barrier, inc=1, device_id={axis: lax.rem(me + k, count)},
+                device_id_type=pl.DeviceIdType.MESH,
+            )
+    pl.semaphore_wait(barrier, t_count + z_count - 2)
+    for axis, count, src, got, snd, rcv in (
+        ("tm", t_count, x_ref, t_got, t_send, t_recv),
+        ("space", z_count, z_own, z_got, z_send, z_recv),
+    ):
+        me = lax.axis_index(axis)
+        made = []
+        for k in range(1, count):
+            made.append(
+                pltpu.make_async_remote_copy(
+                    src_ref=src, dst_ref=got.at[me], send_sem=snd.at[k], recv_sem=rcv.at[k],
+                    device_id={axis: lax.rem(me + k, count)},
+                    device_id_type=pl.DeviceIdType.MESH,
+                )
+            )
+        for copy in made:
+            copy.start()
+        got[me] = src[...]
+        for copy in made:
+            copy.wait()
+        total = got[0]
+        for k in range(1, count):
+            total = total + got[k]
+        if axis == "tm":
+            z_own[...] = total
+        else:
+            out_ref[...] = total
+
+
+def summed(parts):
+    t_count, z_count = lax.axis_size("tm"), lax.axis_size("space")
+    row = lax.broadcasted_iota(jnp.int32, (TILE, LANES), 0)
+    packed = jnp.zeros((TILE, LANES), jnp.float32)
+    for k, part in enumerate(parts):
+        packed = jnp.where(row == k, part, packed)
+    vmem = pl.BlockSpec(memory_space=pltpu.VMEM)
+    dma = pltpu.SemaphoreType.DMA
+    total = pl.pallas_call(
+        functools.partial(sum_kernel, t_count, z_count),
+        out_shape=jax.ShapeDtypeStruct((TILE, LANES), jnp.float32),
+        in_specs=[vmem],
+        out_specs=vmem,
+        scratch_shapes=[
+            pltpu.VMEM((t_count, TILE, LANES), jnp.float32),
+            pltpu.VMEM((TILE, LANES), jnp.float32),
+            pltpu.VMEM((z_count, TILE, LANES), jnp.float32),
+            dma((t_count,)), dma((t_count,)), dma((z_count,)), dma((z_count,)),
+        ],
+        compiler_params=pltpu.CompilerParams(
+            collective_id=2, has_side_effects=True, vmem_limit_bytes=4 * 1024 * 1024
+        ),
+    )(packed)
+    return [total[k, 0] for k in range(len(parts))]
+
+
 def jacobian(values, trajectory, mobility):
     arriving = passed_along(values[-1:], "tm", 1)
     earlier = jnp.concatenate([arriving, values[:-1]], axis=0)
@@ -247,9 +315,8 @@
     frozen = reaction_scale * jnp.maximum(3.0 * initial_state * initial_state - 1.0, 0.0)
     direction = precondition(residual, frozen, mobility, tables)
     applied = jacobian(direction, trajectory, mobility)
-    norm_square, cross_sum, squared_applied = lax.psum(
-        (jnp.sum(residual * residual), jnp.sum(residual * applied), jnp.sum(applied * applied)),
-        ("tm", "space"),
+    norm_square, cross_sum, squared_applied = summed(
+        (jnp.sum(residual * residual), jnp.sum(residual * applied), jnp.sum(applied * applied))
     )
     projection = cross_sum / norm_square
     squared_sum = squared_applied / norm_square

time: 274 us -> 247 us (0.901)
  blocking collectives: 37.1 us -> 0 us
  Pallas kernels: 66.2 us -> 74.5 us
    psum x1 -> x0, blocking collectives: 37.1 us -> none  [on_device(): lax.psum((jnp.sum(residual * residual), jnp.sum(residual * applied), jnp....]
    pallas_call x0 -> x1, Pallas kernels: none -> 8.27 us  [summed(): pl.pallas_call(functools.partial(sum_kernel, t_count, z_count), out_shape...]
where the time goes in v4:
time: 247 us; the launch traced here: 246 us
  waiting for transfers between devices  109 us (44%)
  Pallas kernels  74.5 us (30%)
  starting transfers between devices  20.7 us (8%)
  local copies, waits for them, and re-layouts  15.9 us (6%)
  other arithmetic  15.1 us (6%)
  between operations  7.39 us (3%)
  matrix products  3.9 us (2%)
    pallas_call x1, Pallas kernels, relax_pairs(): pl.pallas_call(functools.partial(relax_kernel, count), out_shape=jax.Shap...  66.2 us
    all_to_all x1, waiting for transfers between devices, precondition(): lax.all_to_all(solved, 'tm', split_axis=1, concat_axis=0, tiled=True)  26.5 us
    all_to_all x1, waiting for transfers between devices, precondition(): lax.all_to_all(weighted, 'tm', split_axis=1, concat_axis=0, tiled=True)  26.3 us
    all_to_all x1, waiting for transfers between devices, precondition(): lax.all_to_all(spectrum, 'tm', split_axis=0, concat_axis=1, tiled=True)  25.8 us
    all_to_all x1, waiting for transfers between devices, precondition(): lax.all_to_all(in_time, 'tm', split_axis=0, concat_axis=1, tiled=True)  24.6 us
    pallas_call x1, Pallas kernels, summed(): pl.pallas_call(functools.partial(sum_kernel, t_count, z_count), out_shape...  8.27 us
    reduce_sum x1, other arithmetic, on_device(): jnp.sum(applied * applied)  6.76 us
    all_to_all x1, starting transfers between devices, precondition(): lax.all_to_all(weighted, 'tm', split_axis=1, concat_axis=0, tiled=True)  5.2 us
  transfers between devices with their start and end apart: 7, of which 6 were waited for; matrix products, arithmetic and copies ran while one was open for 1% of the time, Pallas kernels for 0%

profile of v4, /device:TPU:0, one launch (start us, length us, event | category | flops | bytes accessed | tf_op | source)
XLA Modules:
  0.0 246.3 jit_solution(15403682231192510077)
XLA Ops:
  0.7 4.1 %copy_multiply_fusion = f32[8,64,1024]{2,0,1:T(8,128)} fusion(f32[8,64,1024]{2,1,0:T(8,128)} %param.8, f32[8]{0:T(128)S(1)} %dynamic_slice.11), kind=kLoop, calls=%fused_computation.26 | loop fusion | flops 524288 | bytes 4194336 | tf_op jit(solution)/shard_map/mul | solution.py:219
  4.9 5.2 %all-to-all-start = ((f32[8,64,1024]{2,0,1:T(8,128)}), f32[8,64,1024]{2,0,1:T(8,128)S(1)}, u32[]{:S(2)}, u32[]{:S(2)}) async-start(f32[8,64,1024]{2,0,1:T(8,128)} %copy_multiply_fusion), calls=%async_computation | async-start | bytes 4194304 | tf_op jit(solution)/shard_map/all_to_all | solution.py:223
  10.4 26.3 %all-to-all-done = f32[8,64,1024]{2,0,1:T(8,128)S(1)} async-done(((f32[8,64,1024]{2,0,1:T(8,128)}), f32[8,64,1024]{2,0,1:T(8,128)S(1)}, u32[]{:S(2)}, u32[]{:S(2)}) %all-to-all-start) | async-done | bytes 2097184 | tf_op jit(solution)/shard_map/all_to_all | solution.py:223
  36.7 1.9 fusion.13
  38.6 2.5 %copy.72 = f32[64,8,1024]{2,1,0:T(8,128)} copy(f32[64,8,1024]{2,0,1:T(8,128)S(1)} %fusion.13) | data formatting | bytes 4194304 | tf_op jit(solution)/shard_map/mj,jrc->mrc/dot_general | solution.py:220
  41.2 3.7 %all-to-all-start.1 = ((f32[64,8,1024]{2,1,0:T(8,128)}), f32[64,8,1024]{2,1,0:T(8,128)S(1)}, u32[]{:S(2)}, u32[]{:S(2)}) async-start(f32[64,8,1024]{2,1,0:T(8,128)} %copy.72), calls=%async_computation.1 | async-start | bytes 4194304 | tf_op jit(solution)/shard_map/all_to_all | solution.py:226
  45.7 25.8 %all-to-all-done.1 = f32[64,8,1024]{2,1,0:T(8,128)S(1)} async-done(((f32[64,8,1024]{2,1,0:T(8,128)}), f32[64,8,1024]{2,1,0:T(8,128)S(1)}, u32[]{:S(2)}, u32[]{:S(2)}) %all-to-all-start.1) | async-done | bytes 2097184 | tf_op jit(solution)/shard_map/all_to_all | solution.py:226
  71.6 66.2 %shard_map.59 = f32[8,64,1024]{2,1,0:T(8,128)S(1)} custom-call(f32[8]{0:T(128)S(1)} %dynamic_slice.9.shift_ref, f32[8]{0:T(128)S(1)} %dynamic_slice.10.signed_ref, f32[8,64,1024]{2,1,0:T(8,128)S(1)} %bitcast.37, f32[64,1024]{1,0:T(8,128)S(1)} %fusion.20.base_ref, f32[64,1024]{1,0:T(8,128)S(1)} %copy-done), custom_call_target="tpu_custom_call" | custom-call | tf_op jit(solution)/shard_map/pallas_call | solution.py:190
  137.8 2.5 %copy.74 = f32[8,64,1024]{2,0,1:T(8,128)} copy(f32[8,64,1024]{2,1,0:T(8,128)S(1)} %shard_map.59) | data formatting | bytes 4194304 | tf_op jit(solution)/shard_map/pallas_call | solution.py:190
  140.3 3.6 %all-to-all-start.2 = ((f32[8,64,1024]{2,0,1:T(8,128)}), f32[8,64,1024]{2,0,1:T(8,128)S(1)}, u32[]{:S(2)}, u32[]{:S(2)}) async-start(f32[8,64,1024]{2,0,1:T(8,128)} %copy.74), calls=%async_computation.2 | async-start | bytes 4194304 | tf_op jit(solution)/shard_map/all_to_all | solution.py:231
  144.0 26.5 %all-to-all-done.2 = f32[8,64,1024]{2,0,1:T(8,128)S(1)} async-done(((f32[8,64,1024]{2,0,1:T(8,128)}), f32[8,64,1024]{2,0,1:T(8,128)S(1)}, u32[]{:S(2)}, u32[]{:S(2)}) %all-to-all-start.2) | async-done | bytes 2097184 | tf_op jit(solution)/shard_map/all_to_all | solution.py:231
  170.5 2.0 fusion.11
  172.5 2.5 %copy.77 = f32[64,8,1024]{2,1,0:T(8,128)} copy(f32[64,8,1024]{2,0,1:T(8,128)S(1)} %fusion.11) | data formatting | bytes 4194304 | tf_op jit(solution)/shard_map/jm,mrc->jrc/dot_general | solution.py:228
  175.0 4.7 %all-to-all-start.3 = ((f32[64,8,1024]{2,1,0:T(8,128)}), f32[64,8,1024]{2,1,0:T(8,128)}, u32[]{:S(2)}, u32[]{:S(2)}) async-start(f32[64,8,1024]{2,1,0:T(8,128)} %copy.77), calls=%async_computation.3 | async-start | bytes 4194304 | tf_op jit(solution)/shard_map/all_to_all | solution.py:234
  179.7 1.1 multiply_reduce_fusion
  180.8 0.6 compare_select_fusion
  181.5 24.6 %all-to-all-done.3 = f32[64,8,1024]{2,1,0:T(8,128)} async-done(((f32[64,8,1024]{2,1,0:T(8,128)}), f32[64,8,1024]{2,1,0:T(8,128)}, u32[]{:S(2)}, u32[]{:S(2)}) %all-to-all-start.3) | async-done | bytes 2097184 | tf_op jit(solution)/shard_map/all_to_all | solution.py:234
  206.1 2.8 %copy.78 = f32[8,8,8,1024]{3,1,2,0:T(8,128)S(1)} copy(f32[8,8,8,1024]{3,2,1,0:T(8,128)} %bitcast.13) | data formatting | bytes 4194304 | tf_op jit(solution)/shard_map/all_to_all | solution.py:234
  208.9 0.3 bitcast_divide_fusion
  209.2 0.3 slice.68
  209.5 0.8 fusion.30
  210.4 1.4 collective-permute-start
  211.9 2.1 collective-permute-start.1
  214.1 0.3 copy.80
  214.4 1.6 collective-permute-done.1
  215.9 4.0 %collective-permute-done.2 = f32[8,1,1024]{2,0,1:T(8,128)S(1)} collective-permute-done((f32[8,1,1024]{2,0,1:T(8,128)S(1)}, f32[8,1,1024]{2,0,1:T(8,128)S(1)}, u32[]{:S(2)}, u32[]{:S(2)}) %collective-permute-start.2) | collective-permute-done | bytes 32800 | tf_op jit(solution)/shard_map/ppermute | solution.py:25
  220.0 6.8 %multiply_reduce_fusion.2 = (f32[]{:T(128)}, f32[]{:T(128)}) fusion(f32[8,64,1024]{2,1,0:T(8,128)S(1)} %copy-done.2, f32[8,64,1024]{2,0,1:T(8,128)S(1)} %bitcast_divide_fusion, f32[8,64,1024]{2,1,0:T(8,128)S(1)} %copy-done.3, f32[8,64,1]{2,0,1:T(8,128)S(1)} %get-tuple-element.26, f32[8,64,1023]{2,0,1:T(8,128)S(1)} %get-tuple-element.24, ...), kind=kLoop, calls=%fused_computation.25 | loop fusion | flops 12582910 | bytes 12910600 | tf_op jit(solution)/shard_map/reduce_sum | solution.py:319
  226.7 1.4 select_select_fusion.x_ref
  228.1 8.3 %shard_map.60 = f32[8,128]{1,0:T(8,128)S(1)} custom-call(f32[8,128]{1,0:T(8,128)S(1)} %select_select_fusion.x_ref), custom_call_target="tpu_custom_call" | custom-call | tf_op jit(solution)/shard_map/pallas_call | solution.py:288
  236.4 0.5 fusion.33
  242.3 0.3 broadcast_multiply_fusion
  242.6 2.5 %copy.84 = f32[8,64,1024]{2,1,0:T(8,128)} copy(f32[8,64,1024]{2,0,1:T(8,128)S(1)} %broadcast_multiply_fusion) | data formatting | bytes 4194304
  (41 shorter events, 1.6 us)
Async XLA Ops:
  4.9 31.8 %all-to-all-start = ((f32[8,64,1024]{2,0,1:T(8,128)}), f32[8,64,1024]{2,0,1:T(8,128)S(1)}, u32[]{:S(2)}, u32[]{:S(2)}) async-start(f32[8,64,1024]{2,0,1:T(8,128)} %copy_multiply_fusion), calls=%async_computation | async-start | bytes 4194304 | tf_op jit(solution)/shard_map/all_to_all | solution.py:223
  41.1 4.4 %copy-start = (f32[64,1024]{1,0:T(8,128)S(1)}, f32[64,1024]{1,0:T(8,128)}, u32[]{:S(2)}) copy-start(f32[64,1024]{1,0:T(8,128)} %mob_ref.1) | copy-start | bytes 786436
  41.2 4.4 %copy-start.4 = (f32[64,1024]{1,0:T(8,128)S(1)}, f32[64,1024]{1,0:T(8,128)}, u32[]{:S(2)}) copy-start(f32[64,1024]{1,0:T(8,128)} %param.7) | copy-start | bytes 786436
  41.2 30.3 %all-to-all-start.1 = ((f32[64,8,1024]{2,1,0:T(8,128)}), f32[64,8,1024]{2,1,0:T(8,128)S(1)}, u32[]{:S(2)}, u32[]{:S(2)}) async-start(f32[64,8,1024]{2,1,0:T(8,128)} %copy.72), calls=%async_computation.1 | async-start | bytes 4194304 | tf_op jit(solution)/shard_map/all_to_all | solution.py:226
  140.3 30.2 %all-to-all-start.2 = ((f32[8,64,1024]{2,0,1:T(8,128)}), f32[8,64,1024]{2,0,1:T(8,128)S(1)}, u32[]{:S(2)}, u32[]{:S(2)}) async-start(f32[8,64,1024]{2,0,1:T(8,128)} %copy.74), calls=%async_computation.2 | async-start | bytes 4194304 | tf_op jit(solution)/shard_map/all_to_all | solution.py:231
  175.0 4.7 %copy-start.1 = (f32[8,64,1024]{2,1,0:T(8,128)S(1)}, f32[8,64,1024]{2,1,0:T(8,128)}, u32[]{:S(2)}) copy-start(f32[8,64,1024]{2,1,0:T(8,128)} %param.8) | copy-start | bytes 6291460
  175.0 31.1 %all-to-all-start.3 = ((f32[64,8,1024]{2,1,0:T(8,128)}), f32[64,8,1024]{2,1,0:T(8,128)}, u32[]{:S(2)}, u32[]{:S(2)}) async-start(f32[64,8,1024]{2,1,0:T(8,128)} %copy.77), calls=%async_computation.3 | async-start | bytes 4194304 | tf_op jit(solution)/shard_map/all_to_all | solution.py:234
  209.5 10.5 %copy-start.3 = (f32[8,64,1024]{2,1,0:T(8,128)S(1)}, f32[8,64,1024]{2,1,0:T(8,128)}, u32[]{:S(2)}) copy-start(f32[8,64,1024]{2,1,0:T(8,128)} %param.6) | copy-start | bytes 6291460
  210.3 9.6 %copy-start.2 = (f32[8,64,1024]{2,1,0:T(8,128)S(1)}, f32[8,64,1024]{2,1,0:T(8,128)}, u32[]{:S(2)}) copy-start(f32[8,64,1024]{2,1,0:T(8,128)} %param.8) | copy-start | bytes 6291460
  210.4 3.7 %collective-permute-start = (f32[1,64,1024]{2,1,0:T(8,128)S(1)}, f32[1,64,1024]{2,1,0:T(8,128)S(1)}, u32[]{:S(2)}, u32[]{:S(2)}) collective-permute-start(f32[1,64,1024]{2,1,0:T(8,128)S(1)} %copy.79), channel_id=1, source_target_pairs={{0,4},{4,8},{8,12},{12,16},{16,20},{20,24},{24,28},{1,5},{5,9},{9,... | collective-permute-start | bytes 786440 | tf_op jit(solution)/shard_map/ppermute | solution.py:36
  211.9 4.1 %collective-permute-start.1 = (f32[8,1,1024]{2,0,1:T(8,128)S(1)}, f32[8,1,1024]{2,0,1:T(8,128)S(1)}, u32[]{:S(2)}, u32[]{:S(2)}) collective-permute-start(f32[8,1,1024]{2,0,1:T(8,128)S(1)} %get-tuple-element.28), channel_id=1, source_target_pairs={{1,0},{2,1},{3,2},{0,3},{5,4},{6,5},{7,6},{4,7},{9,8},{10,9},{11,1... | collective-permute-start | bytes 98312 | tf_op jit(solution)/shard_map/ppermute | solution.py:28
  213.9 6.0 %collective-permute-start.2 = (f32[8,1,1024]{2,0,1:T(8,128)S(1)}, f32[8,1,1024]{2,0,1:T(8,128)S(1)}, u32[]{:S(2)}, u32[]{:S(2)}) collective-permute-start(f32[8,1,1024]{2,0,1:T(8,128)S(1)} %get-tuple-element.29), channel_id=1, source_target_pairs={{0,1},{1,2},{2,3},{3,0},{4,5},{5,6},{6,7},{7,4},{8,9},{9,10},{10,1... | collective-permute-start | bytes 98312 | tf_op jit(solution)/shard_map/ppermute | solution.py:25
